TPU v7x, 32 devices: a whole 2x2x4 slice. The times are simulated.
32 devices in a mesh: rep: 4 (over y, x), cp: 8 (over z, core).
Axes of the slice: x: 2, y: 2, z: 4, core: 2. Of those that a mesh axis runs over, the one named last changes fastest.
Arguments:
- tokens: bfloat16 [4, 2048, 768], P('rep', 'cp'), may hold values from -6 to 6
- query_weight: bfloat16 [768, 768], P('cp'), may hold values from -0.3125 to 0.3125
- query_bias: bfloat16 [768], P('cp'), may hold values from -3 to 3
- key_weight: bfloat16 [768, 768], P('cp'), may hold values from -0.3125 to 0.3125
- value_weight: bfloat16 [768, 768], P('cp'), may hold values from -0.21875 to 0.21875
- value_bias: bfloat16 [768], P('cp'), may hold values from -3 to 3
- output_weight: bfloat16 [768, 768], P('cp'), may hold values from -1.5 to 1.5
- output_bias: bfloat16 [768], P('cp'), may hold values from -1.796875 to 1.796875
- first_gain: bfloat16 [768], P('cp'), may hold values from 0.099609375 to 1.8984375
- first_shift: bfloat16 [768], P('cp'), may hold values from -1.796875 to 1.796875
- up_weight: bfloat16 [768, 3072], P('cp'), may hold values from -0.21875 to 0.21875
- up_bias: bfloat16 [3072], P('cp'), may hold values from -3 to 3
- down_weight: bfloat16 [3072, 768], P('cp'), may hold values from -0.109375 to 0.109375
- down_bias: bfloat16 [768], P('cp'), may hold values from -1.796875 to 1.796875
- second_gain: bfloat16 [768], P('cp'), may hold values from 0.099609375 to 1.8984375
- second_shift: bfloat16 [768], P('cp'), may hold values from -1.796875 to 1.796875
- cotangent: float32 [4, 2048, 768], P('rep', 'cp'), may hold values from -18 to 18
Outputs:
- layer_out: float32 [4, 2048, 768], P('rep', 'cp')
- grad_tokens: float32 [4, 2048, 768], P('rep', 'cp')
- grad_query_weight: float32 [768, 768], P('cp')
- grad_query_bias: float32 [768], P('cp')
- grad_key_weight: float32 [768, 768], P('cp')
- grad_value_weight: float32 [768, 768], P('cp')
- grad_value_bias: float32 [768], P('cp')
- grad_output_weight: float32 [768, 768], P('cp')
- grad_output_bias: float32 [768], P('cp')
- grad_first_gain: float32 [768], P('cp')
- grad_first_shift: float32 [768], P('cp')
- grad_up_weight: float32 [768, 3072], P('cp')
- grad_up_bias: float32 [3072], P('cp')
- grad_down_weight: float32 [3072, 768], P('cp')
- grad_down_bias: float32 [768], P('cp')
- grad_second_gain: float32 [768], P('cp')
- grad_second_shift: float32 [768], P('cp')
- rms_values: float32 [1], replicated
All inputs are finite; a program needn't handle non-finite values.
Results may differ from a plain program's by a relative error of at most 0.025.
Values may be sent and summed in bfloat16 or wider, within the bound.
A program may use at most 192 MiB of HBM per device.

v0:
```python
import math

import jax
import jax.numpy as jnp
from jax import lax
from jax.sharding import PartitionSpec as P

H = 12
HD = 64
KEYB = 512


EPSILON = 1e-12


def for_sending(x):
    return jax.tree.map(lambda a: a.astype(jnp.bfloat16) if a.dtype == jnp.float32 else a, x)


def normalize(values, norm_gain, norm_shift):
    center = values - jnp.mean(values, axis=-1, keepdims=True)
    spread = jnp.mean(center * center, axis=-1, keepdims=True)
    return center * lax.rsqrt(spread + EPSILON) * norm_gain + norm_shift


def gelu_exact(values):
    return 0.5 * values * (1.0 + lax.erf(values * (1.0 / math.sqrt(2.0))))


def matmul(left, right):
    return jnp.dot(left, right, preferred_element_type=jnp.float32)


def over_rows(left, right):
    return jnp.einsum("ta,tb->ab", left, right, preferred_element_type=jnp.float32)


def against(left, right):
    return jnp.einsum("ta,ba->tb", left, right, preferred_element_type=jnp.float32)


def column_sum(values):
    return jnp.sum(values.astype(jnp.float32), axis=0)


def head_scores(query_heads, key_heads):
    raw_scores = jnp.einsum(
        "qhd,khd->hqk", query_heads, key_heads, preferred_element_type=jnp.float32
    )
    return raw_scores * (1.0 / math.sqrt(HD))


def probabilities(scores, row_top, row_total):
    return jnp.exp(scores - row_top[:, :, None]) / row_total[:, :, None]


def score_grads(query_heads, grad_heads, key_heads, value_heads, row_top, row_total, row_delta):
    probs = probabilities(head_scores(query_heads, key_heads), row_top, row_total)
    grad_probs = jnp.einsum(
        "qhd,khd->hqk", grad_heads, value_heads, preferred_element_type=jnp.float32
    )
    grad_scores = (probs * (grad_probs - row_delta[:, :, None]) * (1.0 / math.sqrt(HD))).astype(
        jnp.bfloat16
    )
    return (probs.astype(jnp.bfloat16), grad_scores)


def on_device(
    tokens,
    query_weight,
    query_bias,
    key_weight,
    value_weight,
    value_bias,
    output_weight,
    output_bias,
    first_gain,
    first_shift,
    up_weight,
    up_bias,
    down_weight,
    down_bias,
    second_gain,
    second_shift,
    cotangent,
):
    shards = (
        query_weight,
        query_bias,
        key_weight,
        value_weight,
        value_bias,
        output_weight,
        output_bias,
        first_gain,
        first_shift,
        up_weight,
        up_bias,
        down_weight,
        down_bias,
        second_gain,
        second_shift,
    )
    gathered = (
        lax.all_gather(shards[0], "cp", axis=0, tiled=True),
        lax.all_gather(shards[1], "cp", axis=0, tiled=True),
        lax.all_gather(shards[2], "cp", axis=0, tiled=True),
        lax.all_gather(shards[3], "cp", axis=0, tiled=True),
        lax.all_gather(shards[4], "cp", axis=0, tiled=True),
        lax.all_gather(shards[5], "cp", axis=0, tiled=True),
        lax.all_gather(shards[6], "cp", axis=0, tiled=True),
        lax.all_gather(shards[7], "cp", axis=0, tiled=True),
        lax.all_gather(shards[8], "cp", axis=0, tiled=True),
        lax.all_gather(shards[9], "cp", axis=0, tiled=True),
        lax.all_gather(shards[10], "cp", axis=0, tiled=True),
        lax.all_gather(shards[11], "cp", axis=0, tiled=True),
        lax.all_gather(shards[12], "cp", axis=0, tiled=True),
        lax.all_gather(shards[13], "cp", axis=0, tiled=True),
        lax.all_gather(shards[14], "cp", axis=0, tiled=True),
    )
    (
        w_query,
        b_query,
        w_key,
        w_value,
        b_value,
        w_output,
        b_output,
        gain_first,
        shift_first,
        w_up,
        b_up,
        w_down,
        b_down,
        gain_second,
        shift_second,
    ) = gathered
    row_count = tokens.shape[1]
    model_width = tokens.shape[2]
    local_tokens = tokens[0]
    query_rows = (matmul(local_tokens, w_query) + b_query.astype(jnp.float32)).astype(jnp.bfloat16)
    key_rows = matmul(local_tokens, w_key).astype(jnp.bfloat16)
    value_rows = (matmul(local_tokens, w_value) + b_value.astype(jnp.float32)).astype(jnp.bfloat16)
    all_keys, all_values = (
        lax.all_gather(key_rows, "cp", axis=0, tiled=True),
        lax.all_gather(value_rows, "cp", axis=0, tiled=True),
    )
    seq_len = all_keys.shape[0]
    block_len = math.gcd(seq_len, KEYB)
    key_blocks = all_keys.reshape(seq_len // block_len, block_len, H, HD)
    value_blocks = all_values.reshape(seq_len // block_len, block_len, H, HD)
    query_heads = query_rows.reshape(row_count, H, HD)

    def stat_step(carry, key_block):
        old_top, old_total = carry
        scores = head_scores(query_heads, key_block)
        new_top = jnp.maximum(old_top, jnp.max(scores, axis=-1))
        new_total = old_total * jnp.exp(old_top - new_top) + jnp.sum(
            jnp.exp(scores - new_top[:, :, None]), axis=-1
        )
        return ((new_top, new_total), None)

    start_top = jnp.full((H, row_count), -jnp.inf, jnp.float32)
    start_total = jnp.zeros((H, row_count), jnp.float32)
    (row_top, row_total), _ = lax.scan(stat_step, (start_top, start_total), key_blocks)

    def value_step(carry, blocks):
        key_block, value_block = blocks
        probs = probabilities(head_scores(query_heads, key_block), row_top, row_total).astype(
            jnp.bfloat16
        )
        return (
            carry
            + jnp.einsum("hqk,khd->qhd", probs, value_block, preferred_element_type=jnp.float32),
            None,
        )

    head_zeros = jnp.zeros((row_count, H, HD), jnp.float32)
    context, _ = lax.scan(value_step, head_zeros, (key_blocks, value_blocks))
    context_low = context.reshape(row_count, model_width).astype(jnp.bfloat16)
    attn_out = matmul(context_low, w_output) + b_output.astype(jnp.float32)
    resid_first = local_tokens.astype(jnp.float32) + attn_out
    gain_one = gain_first.astype(jnp.float32)
    shift_one = shift_first.astype(jnp.float32)
    first_norm = normalize(resid_first, gain_one, shift_one)
    first_low = first_norm.astype(jnp.bfloat16)
    inner_act = matmul(first_low, w_up) + b_up.astype(jnp.float32)
    hidden_low = gelu_exact(inner_act).astype(jnp.bfloat16)
    resid_second = first_norm + (matmul(hidden_low, w_down) + b_down.astype(jnp.float32))
    gain_two = gain_second.astype(jnp.float32)
    shift_two = shift_second.astype(jnp.float32)
    layer_out = normalize(resid_second, gain_two, shift_two)
    backward_set = (
        lax.all_gather(shards[0], "cp", axis=0, tiled=True),
        lax.all_gather(shards[1], "cp", axis=0, tiled=True),
        lax.all_gather(shards[2], "cp", axis=0, tiled=True),
        lax.all_gather(shards[3], "cp", axis=0, tiled=True),
        lax.all_gather(shards[4], "cp", axis=0, tiled=True),
        lax.all_gather(shards[5], "cp", axis=0, tiled=True),
        lax.all_gather(shards[6], "cp", axis=0, tiled=True),
        lax.all_gather(shards[7], "cp", axis=0, tiled=True),
        lax.all_gather(shards[8], "cp", axis=0, tiled=True),
        lax.all_gather(shards[9], "cp", axis=0, tiled=True),
        lax.all_gather(shards[10], "cp", axis=0, tiled=True),
        lax.all_gather(shards[11], "cp", axis=0, tiled=True),
        lax.all_gather(shards[12], "cp", axis=0, tiled=True),
        lax.all_gather(shards[13], "cp", axis=0, tiled=True),
        lax.all_gather(shards[14], "cp", axis=0, tiled=True),
    )
    (
        back_query,
        back_qbias,
        back_key,
        back_value,
        back_vbias,
        back_output,
        back_obias,
        back_gain1,
        back_shift1,
        back_up,
        back_ubias,
        back_down,
        back_dbias,
        back_gain2,
        back_shift2,
    ) = backward_set
    _, pull_second = jax.vjp(
        normalize, resid_second, back_gain2.astype(jnp.float32), back_shift2.astype(jnp.float32)
    )
    grad_resid2, grad_gain2, grad_shift2 = pull_second(cotangent[0])
    grad_outer = grad_resid2.astype(jnp.bfloat16)
    grad_down_bias = column_sum(grad_outer)
    grad_down_weight = over_rows(hidden_low, grad_outer)
    grad_hidden = against(grad_outer, back_down)
    _, pull_gelu = jax.vjp(gelu_exact, inner_act)
    grad_inner = pull_gelu(grad_hidden)[0].astype(jnp.bfloat16)
    grad_up_bias = column_sum(grad_inner)
    grad_up_weight = over_rows(first_low, grad_inner)
    grad_first = grad_resid2 + against(grad_inner, back_up)
    _, pull_first = jax.vjp(
        normalize, resid_first, back_gain1.astype(jnp.float32), back_shift1.astype(jnp.float32)
    )
    grad_resid1, grad_gain1, grad_shift1 = pull_first(grad_first)
    grad_attn = grad_resid1.astype(jnp.bfloat16)
    grad_output_bias = column_sum(grad_attn)
    grad_output_weight = over_rows(context_low, grad_attn)
    grad_context = against(grad_attn, back_output).astype(jnp.bfloat16)
    grad_heads = grad_context.reshape(row_count, H, HD)
    row_delta = jnp.sum(grad_heads.astype(jnp.float32) * context, axis=-1).T

    def key_step(carry, blocks):
        key_block, value_block = blocks
        probs_low, grad_scores = score_grads(
            query_heads, grad_heads, key_block, value_block, row_top, row_total, row_delta
        )
        new_carry = carry + jnp.einsum(
            "hqk,khd->qhd", grad_scores, key_block, preferred_element_type=jnp.float32
        )
        key_part = jnp.einsum(
            "hqk,qhd->khd", grad_scores, query_heads, preferred_element_type=jnp.float32
        )
        value_part = jnp.einsum(
            "hqk,qhd->khd", probs_low, grad_heads, preferred_element_type=jnp.float32
        )
        joined = jnp.concatenate(
            [key_part.reshape(block_len, model_width), value_part.reshape(block_len, model_width)],
            axis=1,
        )
        return (new_carry, joined)

    grad_query_heads, key_terms = lax.scan(key_step, head_zeros, (key_blocks, value_blocks))
    key_pair = lax.psum_scatter(
        key_terms.reshape(seq_len, 2 * model_width).astype(jnp.bfloat16),
        "cp",
        scatter_dimension=0,
        tiled=True,
    ).astype(jnp.float32)
    grad_key_rows = key_pair[:, :model_width]
    grad_value_rows = key_pair[:, model_width:]
    grad_query_low = grad_query_heads.reshape(row_count, model_width).astype(jnp.bfloat16)
    grad_key_low = grad_key_rows.astype(jnp.bfloat16)
    grad_value_low = grad_value_rows.astype(jnp.bfloat16)
    grad_query_weight = over_rows(local_tokens, grad_query_low)
    grad_query_bias = column_sum(grad_query_low)
    grad_key_weight = over_rows(local_tokens, grad_key_low)
    grad_value_weight = over_rows(local_tokens, grad_value_low)
    grad_value_bias = column_sum(grad_value_low)
    grad_tokens = (
        grad_resid1
        + against(grad_query_low, back_query)
        + against(grad_key_low, back_key)
        + against(grad_value_low, back_value)
    )
    input_sq = jnp.sum(grad_tokens * grad_tokens)
    grads = (
        grad_query_weight,
        grad_query_bias,
        grad_key_weight,
        grad_value_weight,
        grad_value_bias,
        grad_output_weight,
        grad_output_bias,
        grad_gain1,
        grad_shift1,
        grad_up_weight,
        grad_up_bias,
        grad_down_weight,
        grad_down_bias,
        grad_gain2,
        grad_shift2,
    )
    summed = (
        lax.psum_scatter(
            grads[0].astype(jnp.bfloat16), "cp", scatter_dimension=0, tiled=True
        ).astype(jnp.float32),
        lax.psum_scatter(
            grads[1].astype(jnp.bfloat16), "cp", scatter_dimension=0, tiled=True
        ).astype(jnp.float32),
        lax.psum_scatter(
            grads[2].astype(jnp.bfloat16), "cp", scatter_dimension=0, tiled=True
        ).astype(jnp.float32),
        lax.psum_scatter(
            grads[3].astype(jnp.bfloat16), "cp", scatter_dimension=0, tiled=True
        ).astype(jnp.float32),
        lax.psum_scatter(
            grads[4].astype(jnp.bfloat16), "cp", scatter_dimension=0, tiled=True
        ).astype(jnp.float32),
        lax.psum_scatter(
            grads[5].astype(jnp.bfloat16), "cp", scatter_dimension=0, tiled=True
        ).astype(jnp.float32),
        lax.psum_scatter(
            grads[6].astype(jnp.bfloat16), "cp", scatter_dimension=0, tiled=True
        ).astype(jnp.float32),
        lax.psum_scatter(
            grads[7].astype(jnp.bfloat16), "cp", scatter_dimension=0, tiled=True
        ).astype(jnp.float32),
        lax.psum_scatter(
            grads[8].astype(jnp.bfloat16), "cp", scatter_dimension=0, tiled=True
        ).astype(jnp.float32),
        lax.psum_scatter(
            grads[9].astype(jnp.bfloat16), "cp", scatter_dimension=0, tiled=True
        ).astype(jnp.float32),
        lax.psum_scatter(
            grads[10].astype(jnp.bfloat16), "cp", scatter_dimension=0, tiled=True
        ).astype(jnp.float32),
        lax.psum_scatter(
            grads[11].astype(jnp.bfloat16), "cp", scatter_dimension=0, tiled=True
        ).astype(jnp.float32),
        lax.psum_scatter(
            grads[12].astype(jnp.bfloat16), "cp", scatter_dimension=0, tiled=True
        ).astype(jnp.float32),
        lax.psum_scatter(
            grads[13].astype(jnp.bfloat16), "cp", scatter_dimension=0, tiled=True
        ).astype(jnp.float32),
        lax.psum_scatter(
            grads[14].astype(jnp.bfloat16), "cp", scatter_dimension=0, tiled=True
        ).astype(jnp.float32),
    )
    carried = ()
    reduced = jax.tree.map(
        lambda part: part.astype(jnp.float32), lax.psum(for_sending(tuple(summed) + carried), "rep")
    )
    input_total = lax.psum(input_sq, ("rep", "cp"))
    count_entries = lax.axis_size("rep") * lax.axis_size("cp") * row_count * model_width
    rms_values = jnp.sqrt(jnp.stack([input_total / count_entries]))
    return (
        layer_out[None],
        grad_tokens[None],
        reduced[0],
        reduced[1],
        reduced[2],
        reduced[3],
        reduced[4],
        reduced[5],
        reduced[6],
        reduced[7],
        reduced[8],
        reduced[9],
        reduced[10],
        reduced[11],
        reduced[12],
        reduced[13],
        reduced[14],
        rms_values,
    )


def solution(mesh):
    in_specs = (
        P("rep", "cp", None),
        P("cp", None),
        P("cp"),
        P("cp", None),
        P("cp", None),
        P("cp"),
        P("cp", None),
        P("cp"),
        P("cp"),
        P("cp"),
        P("cp", None),
        P("cp"),
        P("cp", None),
        P("cp"),
        P("cp"),
        P("cp"),
        P("rep", "cp", None),
    )
    out_specs = (
        P("rep", "cp", None),
        P("rep", "cp", None),
        P("cp", None),
        P("cp"),
        P("cp", None),
        P("cp", None),
        P("cp"),
        P("cp", None),
        P("cp"),
        P("cp"),
        P("cp"),
        P("cp", None),
        P("cp"),
        P("cp", None),
        P("cp"),
        P("cp"),
        P("cp"),
        P(),
    )
    return jax.shard_map(
        on_device, mesh=mesh, in_specs=in_specs, out_specs=out_specs, check_vma=False
    )
```

profile of v0, /device:TPU:0, one launch (start us, length us, event | category | flops | bytes accessed | tf_op | source)
XLA Modules:
  0.0 778.3 jit_solution(13814633855772910897)
XLA Ops:
  17.3 30.8 %all-reduce.18 = (bf16[768]{0:T(1024)(128)(2,1)S(1)}, bf16[768]{0:T(1024)(128)(2,1)S(1)}, bf16[768]{0:T(1024)(128)(2,1)S(1)}, bf16[768]{0:T(1024)(128)(2,1)S(1)}...) all-reduce(bf16[768]{0:T(1024)(128)(2,1)S(1)} %dynamic-update-slice, ...), channel_id=1, replica_groups=mesh['rep'=4,'cp'=8] {'cp'}, use_global_device_ids=true, to_apply=%add.1 | all-reduce | flops 5376 | bytes 21504
  48.1 2.6 fusion.38
  50.8 8.6 %all-gather.14.cloned.1.call-done = bf16[768,768]{1,0:T(8,128)(2,1)} async-done(((bf16[96,768]{1,0:T(8,128)(2,1)}), bf16[768,768]{1,0:T(8,128)(2,1)}) %all-gather.14.cloned.1.call-update) | async-done | bytes 1179664 | tf_op jit(solution)/shard_map/all_gather | solution.py:107
  59.5 2.5 convolution_convert_fusion.7
  67.2 12.8 %all-gather = bf16[8,1,384]{2,1,0:T(2,128)(2,1)S(1)} all-gather(bf16[1,1,384]{2,1,0:T(2,128)(2,1)S(1)} %reshape.166), channel_id=1, replica_groups=mesh['rep'=4,'cp'=8] {'cp'}, dimensions={0}, use_global_device_ids=true | all-gather | bytes 6912 | tf_op jit(solution)/shard_map/all_gather | solution.py:115
  80.5 3.1 all-gather.18.cloned.1.call-done
  83.6 1.7 fusion.39
  85.5 38.1 %all-gather.12.cloned.1.call-done = bf16[2048,768]{1,0:T(8,128)(2,1)} async-done(((bf16[256,768]{1,0:T(8,128)(2,1)}), bf16[2048,768]{1,0:T(8,128)(2,1)}) %all-gather.12.cloned.1.call-update) | async-done | bytes 3145744 | tf_op jit(solution)/shard_map/all_gather | solution.py:146
  123.6 3.2 copy.60
  126.8 4.0 reshape.138
  130.8 4.5 copy.64
  135.2 27.6 %all-gather.16.cloned.1.call-done = bf16[2048,768]{1,0:T(8,128)(2,1)} async-done(((bf16[256,768]{1,0:T(8,128)(2,1)}), bf16[2048,768]{1,0:T(8,128)(2,1)}) %all-gather.16.cloned.1.call-update) | async-done | bytes 3145744 | tf_op jit(solution)/shard_map/all_gather | solution.py:145
  162.8 3.2 copy.61
  166.0 4.0 reshape.139
  170.0 2.7 copy.65
  172.7 13.2 %while.37 = (s32[]{:T(128)}, f32[12,256]{1,0:T(8,128)S(1)}, f32[12,256]{1,0:T(8,128)}, bf16[4,512,12,64]{1,3,2,0:T(8,128)(2,1)S(1)}, bf16[256,12,64]{0,2,1:T(8,128)(2,1)S(1)}, /*index=5*/s32[]{:T(128)}, s32[]{:T(128)}) while((s32[]{:T(128)}, f32[12,256]{1,0:T(8,128)S(1)}, f32[12,256]{1,0:T(8,128)}, ...), condition=%wide.region_3.4_spmd.clone, body=%wide.region_0.3_spmd.clone.sunk | while | flops 209206272 | bytes 13922404 | solution.py:165
  185.9 16.7 %while.38 = (s32[]{:T(128)}, f32[256,12,64]{0,2,1:T(8,128)}, bf16[4,512,12,64]{1,3,2,0:T(8,128)(2,1)}, bf16[4,512,12,64]{1,3,2,0:T(8,128)(2,1)S(1)}, bf16[256,12...) while((s32[]{:T(128)}, f32[256,12,64]{0,2,1:T(8,128)}, ...), condition=%wide.region_5.6_spmd.clone, body=%wide.region_4.5_spmd.clone.sunk | while | flops 409337856 | bytes 3573358 | solution.py:179
  185.9 3.9 fusion.124
  189.8 4.2 fusion.124
  194.0 4.3 fusion.124
  198.4 4.2 fusion.124
  202.6 2.5 convert_element_type.222
  205.1 2.9 fusion.63
  211.0 27.6 %all-gather.22.cloned.1.call-done = bf16[768,3072]{1,0:T(8,128)(2,1)} async-done(((bf16[96,3072]{1,0:T(8,128)(2,1)}), bf16[768,3072]{1,0:T(8,128)(2,1)}) %all-gather.22.cloned.1.call-update) | async-done | bytes 4718608 | tf_op jit(solution)/shard_map/all_gather | solution.py:114
  238.6 6.6 multiply_convert_fusion.1
  245.1 45.1 %all-gather.24.cloned.1.call-done = bf16[3072,768]{1,0:T(8,128)(2,1)} async-done(((bf16[384,768]{1,0:T(8,128)(2,1)}), bf16[3072,768]{1,0:T(8,128)(2,1)}) %all-gather.24.cloned.1.call-update) | async-done | bytes 4718608 | tf_op jit(solution)/shard_map/all_gather | solution.py:116
  290.2 4.7 fusion.64
  297.2 3.6 fusion.57
  300.8 4.0 multiply_reduce_fusion.1
  309.3 46.7 %while.39 = (s32[]{:T(128)}, f32[256,12,64]{0,2,1:T(8,128)S(1)}, bf16[4,512,1536]{2,1,0:T(8,128)(2,1)}, bf16[4,512,12,64]{1,3,2,0:T(8,128)(2,1)}, bf16[256,12,64...) while((s32[]{:T(128)}, f32[256,12,64]{0,2,1:T(8,128)S(1)}, ...), condition=%wide.region_16.17_spmd.clone, body=%wide.region_15.16_spmd.clone.sunk | while | flops 1022754816 | bytes 54309124 | solution.py:271
  309.3 2.7 exponential_divide_fusion.2
  313.1 2.3 multiply_convert_fusion.3
  315.5 1.8 fusion.135
  321.0 2.7 exponential_divide_fusion.2
  324.8 2.3 multiply_convert_fusion.3
  327.2 1.8 fusion.135
  332.7 2.7 exponential_divide_fusion.2
  336.5 2.3 multiply_convert_fusion.3
  338.8 1.8 fusion.135
  344.4 2.7 exponential_divide_fusion.2
  348.2 2.3 multiply_convert_fusion.3
  350.5 1.8 fusion.135
  359.1 65.7 %reduce-scatter.14.cloned.1.call-done = bf16[256,1536]{1,0:T(8,128)(2,1)} async-done(((bf16[2048,1536]{1,0:T(8,128)(2,1)}), bf16[256,1536]{1,0:T(8,128)(2,1)}) %reduce-scatter.14.cloned.1.call-update) | async-done | bytes 786448 | tf_op jit(solution)/shard_map/reduce_scatter | solution.py:272
  431.9 4.9 convolution_convert_fusion.1
  438.2 3.6 convolution_convert_fusion
  441.9 16.9 %reduce-scatter.22.cloned.1.call-done = bf16[96,768]{1,0:T(8,128)(2,1)} async-done(((bf16[768,768]{1,0:T(8,128)(2,1)}), bf16[96,768]{1,0:T(8,128)(2,1)}) %reduce-scatter.22.cloned.1.call-update) | async-done | bytes 147472
  458.9 1.7 copy.74
  460.6 31.8 %reduce-scatter.26.cloned.1.call-done = bf16[96,768]{1,0:T(8,128)(2,1)} async-done(((bf16[768,768]{1,0:T(8,128)(2,1)}), bf16[96,768]{1,0:T(8,128)(2,1)}) %reduce-scatter.26.cloned.1.call-update) | async-done | bytes 147472
  492.4 1.7 copy.78
  494.1 32.0 %reduce-scatter.24.cloned.1.call-done = bf16[96,768]{1,0:T(8,128)(2,1)} async-done(((bf16[768,768]{1,0:T(8,128)(2,1)}), bf16[96,768]{1,0:T(8,128)(2,1)}) %reduce-scatter.24.cloned.1.call-update) | async-done | bytes 147472
  526.1 1.7 copy.76
  527.8 31.8 %reduce-scatter.16.cloned.1.call-done = bf16[96,768]{1,0:T(8,128)(2,1)} async-done(((bf16[768,768]{1,0:T(8,128)(2,1)}), bf16[96,768]{1,0:T(8,128)(2,1)}) %reduce-scatter.16.cloned.1.call-update) | async-done | bytes 147472 | tf_op jit(solution)/shard_map/reduce_scatter | solution.py:328
  559.6 55.3 %reduce-scatter.18.cloned.1.call-done = bf16[96,3072]{1,0:T(8,128)(2,1)} async-done(((bf16[768,3072]{1,0:T(8,128)(2,1)}), bf16[96,3072]{1,0:T(8,128)(2,1)}) %reduce-scatter.18.cloned.1.call-update) | async-done | bytes 589840 | tf_op jit(solution)/shard_map/reduce_scatter | solution.py:340
  614.9 55.5 %reduce-scatter.20.cloned.1.call-done = bf16[384,768]{1,0:T(8,128)(2,1)} async-done(((bf16[3072,768]{1,0:T(8,128)(2,1)}), bf16[384,768]{1,0:T(8,128)(2,1)}) %reduce-scatter.20.cloned.1.call-update) | async-done | bytes 589840 | tf_op jit(solution)/shard_map/reduce_scatter | solution.py:346
  673.3 2.0 convolution_add_fusion.3
  676.0 2.0 multiply_reduce_fusion
  677.9 38.4 %psum.127 = f32[]{:T(128)} all-reduce(f32[]{:T(128)} %get-tuple-element.440), channel_id=1, replica_groups=mesh['rep'=4,'cp'=8] {'rep','cp'}, use_global_device_ids=true, to_apply=%region_58.59 | all-reduce | flops 1 | bytes 8 | tf_op jit(solution)/shard_map/psum | solution.py:363
  717.2 26.8 %all-reduce.17 = (bf16[768]{0:T(1024)(128)(2,1)S(1)}, bf16[768]{0:T(1024)(128)(2,1)S(1)}, bf16[768]{0:T(1024)(128)(2,1)S(1)}, bf16[768]{0:T(1024)(128)(2,1)S(1)}...) all-reduce(bf16[768]{0:T(1024)(128)(2,1)S(1)} %copy-done.53, ...), channel_id=1, replica_groups=mesh['rep'=4,'cp'=8] {'cp'}, use_global_device_ids=true, to_apply=%add.7 | all-reduce | flops 9984 | bytes 39936
  744.7 9.9 %all-reduce.19 = (bf16[96]{0:T(256)(128)(2,1)S(1)}, bf16[96]{0:T(256)(128)(2,1)S(1)}, bf16[96]{0:T(256)(128)(2,1)S(1)}, bf16[96]{0:T(256)(128)(2,1)S(1)}, bf16[9...) all-reduce(bf16[96]{0:T(256)(128)(2,1)S(1)} %dynamic-slice.9, ...), channel_id=1, replica_groups=mesh['rep'=4,'cp'=8] {'rep'}, use_global_device_ids=true, to_apply=%region_22.23 | all-reduce | flops 1152 | bytes 4608 | tf_op jit(solution)/shard_map/psum | solution.py:361
  760.4 1.8 copy.70
  762.2 1.8 copy.71
  763.9 1.8 copy.72
  765.7 1.6 convert_element_type.254
  767.4 2.2 convert_element_type.261
  (312 shorter events, 78.2 us)
Async XLA Ops:
  7.2 52.3 %copy-start.8 = (bf16[1,256,768]{2,1,0:T(8,128)(2,1)S(1)}, bf16[1,256,768]{2,1,0:T(8,128)(2,1)}, u32[]{:S(2)}) copy-start(bf16[1,256,768]{2,1,0:T(8,128)(2,1)} %param.23) | copy-start | bytes 1179652
  7.2 40.9 %all-gather.10.cloned.1.call-start = ((), (), s32[]{:S(2)}) async-start(), calls=%async_computation.7 | async-start | bytes 1327104 | tf_op jit(solution)/shard_map/all_gather | solution.py:108
  7.9 51.5 %all-gather.14.cloned.1.call-start = ((), (), s32[]{:S(2)}) async-start(), calls=%async_computation.9 | async-start | bytes 1327104 | tf_op jit(solution)/shard_map/all_gather | solution.py:107
  8.7 74.9 %all-gather.18.cloned.1.call-start = ((), (), s32[]{:S(2)}) async-start(), calls=%async_computation.11 | async-start | bytes 1327104 | tf_op jit(solution)/shard_map/all_gather | solution.py:105
  9.4 114.2 %all-gather.12.cloned.1.call-start = ((), (), s32[]{:S(2)}) async-start(), calls=%async_computation.8 | async-start | bytes 3538944 | tf_op jit(solution)/shard_map/all_gather | solution.py:146
  48.1 16.0 %copy-start.57 = (bf16[384]{0:T(512)(128)(2,1)S(1)}, bf16[384]{0:T(512)(128)(2,1)}, u32[]{:S(2)}) copy-start(bf16[384]{0:T(512)(128)(2,1)} %param.34) | copy-start | bytes 2308
  50.8 112.0 %all-gather.16.cloned.1.call-start = ((), (), s32[]{:S(2)}) async-start(), calls=%async_computation.10 | async-start | bytes 3538944 | tf_op jit(solution)/shard_map/all_gather | solution.py:145
  62.0 143.1 %all-gather.20.cloned.1.call-start = ((), (), s32[]{:S(2)}) async-start(), calls=%async_computation.12 | async-start | bytes 1327104 | tf_op jit(solution)/shard_map/all_gather | solution.py:110
  62.6 176.0 %all-gather.22.cloned.1.call-start = ((), (), s32[]{:S(2)}) async-start(), calls=%async_computation.13 | async-start | bytes 5308416 | tf_op jit(solution)/shard_map/all_gather | solution.py:114
  63.3 226.9 %all-gather.24.cloned.1.call-start = ((), (), s32[]{:S(2)}) async-start(), calls=%async_computation.14 | async-start | bytes 5308416 | tf_op jit(solution)/shard_map/all_gather | solution.py:116
  64.1 360.7 %reduce-scatter.14.cloned.1.call-start = ((), (), s32[]{:S(2)}) async-start(), calls=%async_computation.15 | async-start | bytes 7077888 | tf_op jit(solution)/shard_map/reduce_scatter | solution.py:272
  202.6 92.3 %copy-start.2 = (bf16[4,512,12,64]{1,3,2,0:T(8,128)(2,1)}, bf16[4,512,12,64]{1,3,2,0:T(8,128)(2,1)S(1)}, u32[]{:S(2)}) copy-start(bf16[4,512,12,64]{1,3,2,0:T(8,128)(2,1)S(1)} %get-tuple-element.695) | copy-start | bytes 9437188
  290.2 6.9 slice-start.2
  290.2 4.9 copy-start.10
  290.2 5.0 copy-start.32
  290.2 6.9 slice-start.3
  294.9 2.2 copy-start.59
  296.4 4.4 slice-start
  297.1 3.7 copy-start.23
  297.1 3.7 copy-start.29
  297.1 3.7 copy-start.37
  297.1 3.7 copy-start.41
  297.2 3.7 slice-start.1
  300.8 4.0 copy-start.25
  300.8 4.0 copy-start.44
  304.8 3.1 copy-start.16
  304.8 3.8 copy-start.22
  306.4 2.9 copy-start.3
  309.3 8.0 %copy-start = (bf16[256,12,64]{0,2,1:T(8,128)(2,1)}, bf16[256,12,64]{0,2,1:T(8,128)(2,1)S(1)}, u32[]{:S(2)}) copy-start(bf16[256,12,64]{0,2,1:T(8,128)(2,1)S(1)} %get-tuple-element.657) | copy-start | bytes 1179652 | tf_op jit(solution)/shard_map/while
  321.0 8.0 %copy-start = (bf16[256,12,64]{0,2,1:T(8,128)(2,1)}, bf16[256,12,64]{0,2,1:T(8,128)(2,1)S(1)}, u32[]{:S(2)}) copy-start(bf16[256,12,64]{0,2,1:T(8,128)(2,1)S(1)} %get-tuple-element.657) | copy-start | bytes 1179652 | tf_op jit(solution)/shard_map/while
  332.7 8.0 %copy-start = (bf16[256,12,64]{0,2,1:T(8,128)(2,1)}, bf16[256,12,64]{0,2,1:T(8,128)(2,1)S(1)}, u32[]{:S(2)}) copy-start(bf16[256,12,64]{0,2,1:T(8,128)(2,1)S(1)} %get-tuple-element.657) | copy-start | bytes 1179652 | tf_op jit(solution)/shard_map/while
  344.4 8.0 %copy-start = (bf16[256,12,64]{0,2,1:T(8,128)(2,1)}, bf16[256,12,64]{0,2,1:T(8,128)(2,1)S(1)}, u32[]{:S(2)}) copy-start(bf16[256,12,64]{0,2,1:T(8,128)(2,1)S(1)} %get-tuple-element.657) | copy-start | bytes 1179652 | tf_op jit(solution)/shard_map/while
  356.1 102.8 %reduce-scatter.22.cloned.1.call-start = ((), (), s32[]{:S(2)}) async-start(), calls=%async_computation.19 | async-start | bytes 1327104
  359.0 133.4 %reduce-scatter.26.cloned.1.call-start = ((), (), s32[]{:S(2)}) async-start(), calls=%async_computation.21 | async-start | bytes 1327104
  424.7 3.2 copy-start.14
  427.9 98.3 %reduce-scatter.24.cloned.1.call-start = ((), (), s32[]{:S(2)}) async-start(), calls=%async_computation.20 | async-start | bytes 1327104
  428.4 3.4 copy-start.30
  428.5 3.4 copy-start.31
  428.5 3.4 copy-start.38
  428.5 3.4 copy-start.42
  430.0 129.7 %reduce-scatter.16.cloned.1.call-start = ((), (), s32[]{:S(2)}) async-start(), calls=%async_computation.16 | async-start | bytes 1327104 | tf_op jit(solution)/shard_map/reduce_scatter | solution.py:328
  431.5 183.4 %reduce-scatter.18.cloned.1.call-start = ((), (), s32[]{:S(2)}) async-start(), calls=%async_computation.17 | async-start | bytes 5308416 | tf_op jit(solution)/shard_map/reduce_scatter | solution.py:340
  436.8 233.7 %reduce-scatter.20.cloned.1.call-start = ((), (), s32[]{:S(2)}) async-start(), calls=%async_computation.18 | async-start | bytes 5308416 | tf_op jit(solution)/shard_map/reduce_scatter | solution.py:346
  441.9 229.9 %copy-start.11 = (f32[1,256,768]{2,1,0:T(8,128)S(1)}, f32[1,256,768]{2,1,0:T(8,128)}, u32[]{:S(2)}) copy-start(f32[1,256,768]{2,1,0:T(8,128)} %param.39) | copy-start | bytes 2359300
  441.9 230.6 %copy-start.58 = (bf16[96]{0:T(256)(128)(2,1)S(1)}, bf16[96]{0:T(256)(128)(2,1)}, u32[]{:S(2)}) copy-start(bf16[96]{0:T(256)(128)(2,1)} %param.38) | copy-start | bytes 580
  441.9 231.4 %copy-start.13 = (f32[256,768]{1,0:T(8,128)S(1)}, f32[256,768]{1,0:T(8,128)}, u32[]{:S(2)}) copy-start(f32[256,768]{1,0:T(8,128)} %copy-done.12) | copy-start | bytes 2359300
  441.9 231.4 %copy-start.46 = (f32[256]{0:T(256)S(1)}, f32[256]{0:T(256)}, u32[]{:S(2)}) copy-start(f32[256]{0:T(256)} %copy-done.45) | copy-start | bytes 3076
  441.9 318.4 %all-reduce.23.cloned.1.call-start = ((), (), s32[]{:S(2)}) async-start(), calls=%async_computation.22 | async-start | bytes 3833856 | tf_op jit(solution)/shard_map/psum | solution.py:361
  494.1 181.2 %copy-start.15 = (bf16[768,768]{1,0:T(8,128)(2,1)S(1)}, bf16[768,768]{1,0:T(8,128)(2,1)}, u32[]{:S(2)}) copy-start(bf16[768,768]{1,0:T(8,128)(2,1)} %all-gather.14.cloned.1.call-done) | copy-start | bytes 3538948
  673.3 2.6 copy-start.27
  675.3 41.8 %copy-start.47 = (bf16[768]{0:T(1024)(128)(2,1)S(1)}, bf16[768]{0:T(1024)(128)(2,1)}, u32[]{:S(2)}) copy-start(bf16[768]{0:T(1024)(128)(2,1)} %get-tuple-element.336) | copy-start | bytes 4612
  675.3 83.9 %copy-start.7 = (f32[256,768]{1,0:T(8,128)S(1)}, f32[256,768]{1,0:T(8,128)}, u32[]{:S(2)}) copy-start(f32[256,768]{1,0:T(8,128)} %copy-done.6) | copy-start | bytes 2359300
  675.3 83.9 %copy-start.33 = (f32[768]{0:T(1024)S(1)}, f32[768]{0:T(1024)}, u32[]{:S(2)}) copy-start(f32[768]{0:T(1024)} %convert_element_type.231) | copy-start | bytes 9220
  675.3 83.9 %copy-start.35 = (f32[256]{0:T(256)S(1)}, f32[256]{0:T(256)}, u32[]{:S(2)}) copy-start(f32[256]{0:T(256)} %copy-done.34) | copy-start | bytes 3076
  675.3 83.9 %copy-start.40 = (f32[256]{0:T(256)S(1)}, f32[256]{0:T(256)}, u32[]{:S(2)}) copy-start(f32[256]{0:T(256)} %copy-done.39) | copy-start | bytes 3076
  675.9 41.3 %copy-start.48 = (bf16[768]{0:T(1024)(128)(2,1)S(1)}, bf16[768]{0:T(1024)(128)(2,1)}, u32[]{:S(2)}) copy-start(bf16[768]{0:T(1024)(128)(2,1)} %get-tuple-element.417) | copy-start | bytes 4612
  675.9 41.3 %copy-start.49 = (bf16[768]{0:T(1024)(128)(2,1)S(1)}, bf16[768]{0:T(1024)(128)(2,1)}, u32[]{:S(2)}) copy-start(bf16[768]{0:T(1024)(128)(2,1)} %get-tuple-element.421) | copy-start | bytes 4612
  675.9 41.3 %copy-start.50 = (bf16[768]{0:T(1024)(128)(2,1)S(1)}, bf16[768]{0:T(1024)(128)(2,1)}, u32[]{:S(2)}) copy-start(bf16[768]{0:T(1024)(128)(2,1)} %reduce_sum.263) | copy-start | bytes 4612
  675.9 41.3 %copy-start.51 = (bf16[768]{0:T(1024)(128)(2,1)S(1)}, bf16[768]{0:T(1024)(128)(2,1)}, u32[]{:S(2)}) copy-start(bf16[768]{0:T(1024)(128)(2,1)} %reduce_sum.224) | copy-start | bytes 4612
  675.9 41.3 %copy-start.53 = (bf16[768]{0:T(1024)(128)(2,1)S(1)}, bf16[768]{0:T(1024)(128)(2,1)}, u32[]{:S(2)}) copy-start(bf16[768]{0:T(1024)(128)(2,1)} %copy-done.52) | copy-start | bytes 4612
  675.9 41.3 %copy-start.54 = (bf16[3072]{0:T(1024)(128)(2,1)S(1)}, bf16[3072]{0:T(1024)(128)(2,1)}, u32[]{:S(2)}) copy-start(bf16[3072]{0:T(1024)(128)(2,1)} %get-tuple-element.419) | copy-start | bytes 18436
  675.9 41.3 %copy-start.55 = (bf16[768]{0:T(1024)(128)(2,1)S(1)}, bf16[768]{0:T(1024)(128)(2,1)}, u32[]{:S(2)}) copy-start(bf16[768]{0:T(1024)(128)(2,1)} %get-tuple-element.338) | copy-start | bytes 4612
  675.9 41.3 %copy-start.56 = (bf16[768]{0:T(1024)(128)(2,1)S(1)}, bf16[768]{0:T(1024)(128)(2,1)}, u32[]{:S(2)}) copy-start(bf16[768]{0:T(1024)(128)(2,1)} %get-tuple-element.340) | copy-start | bytes 4612
  760.3 9.2 %copy-start.28 = (bf16[384,768]{1,0:T(8,128)(2,1)S(1)}, bf16[384,768]{1,0:T(8,128)(2,1)}, u32[]{:S(2)}) copy-start(bf16[384,768]{1,0:T(8,128)(2,1)} %get-tuple-element.416) | copy-start | bytes 1769476
  (28 other events, 35.7 us)
Sparse Core Ops, SparseCore 0:
  9.6 25.6 all-gather.9
  36.9 22.4 all-gather.13
  61.1 22.4 all-gather.17
  85.7 37.8 all-gather.11
  125.7 37.1 all-gather.15
  164.3 21.6 all-gather.19
  187.7 50.8 all-gather.21
  240.2 49.9 all-gather.23
  356.2 68.4 reduce-scatter.13
  427.4 31.3 reduce-scatter.21
  461.2 31.1 reduce-scatter.25
  495.1 30.9 reduce-scatter.23
  528.4 31.1 reduce-scatter.15
  561.8 53.0 reduce-scatter.17
  617.1 53.3 reduce-scatter.19
  674.7 66.5 all-reduce.22
where the time goes:
time: 780 us; the launch traced here: 778 us
  waiting for transfers between devices  443 us (57%)
  blocking collectives  119 us (15%)
  matrix products  103 us (13%)
  local copies, waits for them, and re-layouts  59.7 us (8%)
  other arithmetic  34 us (4%)
  between operations  18.6 us (2%)
    unnamed x19, waiting for transfers between devices  84.9 us
    reduce_scatter x1, waiting for transfers between devices, on_device(): lax.psum_scatter(key_terms.reshape(seq_len, 2 * model_width).astype(jnp.b...  65.7 us
    unnamed x2, blocking collectives  57.6 us
    reduce_scatter x1, waiting for transfers between devices, on_device(): lax.psum_scatter(grads[11].astype(jnp.bfloat16), 'cp', scatter_dimension=...  55.5 us
    reduce_scatter x1, waiting for transfers between devices, on_device(): lax.psum_scatter(grads[9].astype(jnp.bfloat16), 'cp', scatter_dimension=0...  55.3 us
    all_gather x1, waiting for transfers between devices, on_device(): lax.all_gather(shards[11], 'cp', axis=0, tiled=True)  45.1 us
    psum x1, blocking collectives, on_device(): input_total = lax.psum(input_sq, ('rep', 'cp'))  38.4 us
    all_gather x1, waiting for transfers between devices, on_device(): lax.all_gather(value_rows, 'cp', axis=0, tiled=True)  38.1 us
  transfers between devices with their start and end apart: 16, of which 13 were waited for; matrix products, arithmetic and copies ran while one was open for 15% of the time, Pallas kernels for 0%

commit v1 on v0

v1 whole, which is shorter than its diff:
```python
import math

import jax
import jax.numpy as jnp
from jax import lax
from jax.experimental import pallas as pl
from jax.experimental.pallas import tpu as pltpu
from jax.sharding import PartitionSpec as P

HD = 64
PAIR = 2 * HD
CHUNKS = 3
EPSILON = 1e-12
BF16 = jnp.bfloat16
F32 = jnp.float32
BOTH = ("cp", "rep")


def normalize(values, norm_gain, norm_shift):
    center = values - jnp.mean(values, axis=-1, keepdims=True)
    spread = jnp.mean(center * center, axis=-1, keepdims=True)
    return center * lax.rsqrt(spread + EPSILON) * norm_gain + norm_shift


def gelu_exact(values):
    return 0.5 * values * (1.0 + lax.erf(values * (1.0 / math.sqrt(2.0))))


def matmul(left, right):
    return jnp.dot(left, right, preferred_element_type=F32)


def over_rows(left, right):
    return lax.dot_general(left, right, (((0,), (0,)), ((), ())), preferred_element_type=F32)


def against(left, right):
    return lax.dot_general(left, right, (((1,), (1,)), ((), ())), preferred_element_type=F32)


def column_sum(values):
    return jnp.sum(values.astype(F32), axis=0)


def head_mask(shape, head):
    lane = lax.broadcasted_iota(jnp.int32, shape, 1)
    return (lane >= head * HD) & (lane < (head + 1) * HD)


def forward_kernel(query_ref, pair_ref, context_ref):
    keys = pair_ref[:, :PAIR]
    values = pair_ref[:, PAIR:]
    query = query_ref[...]
    total = None
    for head in range(2):
        mask = head_mask(query.shape, head)
        scores = against(jnp.where(mask, query, jnp.zeros_like(query)), keys)
        top = jnp.max(scores, axis=-1, keepdims=True)
        weight = jnp.exp(scores - top)
        inverse = 1.0 / jnp.sum(weight, axis=-1, keepdims=True)
        part = matmul((weight * inverse).astype(BF16), values)
        total = part if head == 0 else jnp.where(mask, part, total)
    context_ref[...] = total.astype(BF16)


def backward_kernel(query_ref, grad_ref, pair_ref, grad_query_ref, grad_pair_ref):
    keys = pair_ref[:, :PAIR]
    values = pair_ref[:, PAIR:]
    query = query_ref[...]
    grad = grad_ref[...]
    zeros = jnp.zeros_like(query)
    key_part = value_part = query_part = None
    for head in range(2):
        mask = head_mask(query.shape, head)
        own_query = jnp.where(mask, query, zeros)
        own_grad = jnp.where(mask, grad, zeros)
        scores = against(keys, own_query)
        top = jnp.max(scores, axis=0, keepdims=True)
        weight = jnp.exp(scores - top)
        inverse = 1.0 / jnp.sum(weight, axis=0, keepdims=True)
        probs = weight * inverse
        grad_probs = against(values, own_grad)
        delta = jnp.sum(probs * grad_probs, axis=0, keepdims=True)
        grad_scores = (probs * (grad_probs - delta)).astype(BF16)
        new_value = matmul(probs.astype(BF16), own_grad)
        new_key = matmul(grad_scores, own_query)
        new_query = over_rows(keys, grad_scores)
        if head == 0:
            key_part, value_part, query_part = new_key, new_value, new_query
        else:
            key_part = key_part + new_key
            value_part = value_part + new_value
            row = lax.broadcasted_iota(jnp.int32, new_query.shape, 0)
            query_part = jnp.where(row < HD, query_part, new_query)
    grad_query_ref[...] = (query_part.T * (1.0 / math.sqrt(HD))).astype(BF16)
    grad_pair_ref[:, :PAIR] = key_part.astype(BF16)
    grad_pair_ref[:, PAIR:] = value_part.astype(BF16)


def column_block(rows, width):
    return pl.BlockSpec((rows, width), lambda i: (0, i))


def attend(query, pairs):
    rows, width = query.shape
    keys = pairs.shape[0]
    return pl.pallas_call(
        forward_kernel,
        grid=(width // PAIR,),
        in_specs=[column_block(rows, PAIR), column_block(keys, 2 * PAIR)],
        out_specs=column_block(rows, PAIR),
        out_shape=jax.ShapeDtypeStruct((rows, width), BF16),
    )(query, pairs)


def attend_back(query, grad, pairs):
    rows, width = query.shape
    keys = pairs.shape[0]
    return pl.pallas_call(
        backward_kernel,
        grid=(width // PAIR,),
        in_specs=[
            column_block(rows, PAIR),
            column_block(rows, PAIR),
            column_block(keys, 2 * PAIR),
        ],
        out_specs=(column_block(rows, PAIR), column_block(keys, 2 * PAIR)),
        out_shape=(
            jax.ShapeDtypeStruct((rows, width), BF16),
            jax.ShapeDtypeStruct((keys, 2 * width), BF16),
        ),
    )(query, grad, pairs)


def mixed(left, right):
    rows, width = left.shape
    joined = jnp.stack(
        [left.reshape(rows, width // PAIR, PAIR), right.reshape(rows, width // PAIR, PAIR)], axis=2
    )
    return joined.reshape(rows, 2 * width)


def unmixed(both):
    rows, width = both.shape
    parts = both.reshape(rows, width // (2 * PAIR), 2, PAIR)
    return parts[:, :, 0].reshape(rows, width // 2), parts[:, :, 1].reshape(rows, width // 2)


def own_rows(shard):
    share = shard.shape[0] // lax.axis_size("rep")
    return lax.dynamic_slice_in_dim(shard, lax.axis_index("rep") * share, share, 0)


def gather_all(shard):
    return lax.all_gather(own_rows(shard), BOTH, axis=0, tiled=True)


def scatter_all(values):
    return lax.psum_scatter(values.astype(BF16), BOTH, scatter_dimension=0, tiled=True)


def on_device(
    tokens,
    query_weight,
    query_bias,
    key_weight,
    value_weight,
    value_bias,
    output_weight,
    output_bias,
    first_gain,
    first_shift,
    up_weight,
    up_bias,
    down_weight,
    down_bias,
    second_gain,
    second_shift,
    cotangent,
):
    row_count = tokens.shape[1]
    width = tokens.shape[2]
    local_tokens = tokens[0]
    w_proj = gather_all(
        jnp.concatenate([query_weight, mixed(key_weight, value_weight)], axis=1)
    )
    small = (
        query_bias,
        value_bias,
        output_bias,
        first_gain,
        first_shift,
        up_bias,
        down_bias,
        second_gain,
        second_shift,
    )
    gathered = lax.all_gather(jnp.concatenate(small)[None], "cp", axis=0, tiled=True)
    vectors = []
    at = 0
    for vector in small:
        part = gathered[:, at : at + vector.shape[0]]
        vectors.append(part.reshape(-1).astype(F32))
        at += vector.shape[0]
    b_query, b_value, b_output, gain_one, shift_one, b_up, b_down, gain_two, shift_two = vectors
    w_pair = w_proj[:, width:]
    pair_bias = mixed(jnp.zeros_like(b_value)[None], b_value[None])
    pair_rows = (matmul(local_tokens, w_pair) + pair_bias).astype(BF16)
    chunk = width // CHUNKS
    pairs = [
        lax.all_gather(
            pair_rows[:, 2 * chunk * i : 2 * chunk * (i + 1)], "cp", axis=0, tiled=True
        )
        for i in range(CHUNKS)
    ]
    query_rows = (matmul(local_tokens, w_proj[:, :width]) + b_query).astype(BF16)
    query_scaled = query_rows * jnp.asarray(1.0 / math.sqrt(HD), BF16)
    queries = [query_scaled[:, chunk * i : chunk * (i + 1)] for i in range(CHUNKS)]
    w_wide = gather_all(jnp.concatenate([output_weight, up_weight], axis=1))
    w_output = w_wide[:, :width]
    w_up = w_wide[:, width:]
    w_down = gather_all(down_weight)

    context_low = jnp.concatenate(
        [attend(query, pair) for query, pair in zip(queries, pairs)], axis=1
    )
    attn_out = matmul(context_low, w_output) + b_output
    resid_first = local_tokens.astype(F32) + attn_out
    first_norm, pull_first = jax.vjp(normalize, resid_first, gain_one, shift_one)
    first_low = first_norm.astype(BF16)
    inner_act = matmul(first_low, w_up) + b_up
    hidden, pull_gelu = jax.vjp(gelu_exact, inner_act)
    hidden_low = hidden.astype(BF16)
    resid_second = first_norm + (matmul(hidden_low, w_down) + b_down)
    layer_out, pull_second = jax.vjp(normalize, resid_second, gain_two, shift_two)

    grad_resid2, grad_gain2, grad_shift2 = pull_second(cotangent[0])
    grad_outer = grad_resid2.astype(BF16)
    grad_down_bias = column_sum(grad_outer)
    part_down = scatter_all(over_rows(hidden_low, grad_outer))
    grad_inner = pull_gelu(against(grad_outer, w_down))[0].astype(BF16)
    grad_up_bias = column_sum(grad_inner)
    part_up = scatter_all(over_rows(first_low, grad_inner))
    grad_first = grad_resid2 + against(grad_inner, w_up)
    grad_resid1, grad_gain1, grad_shift1 = pull_first(grad_first)
    grad_attn = grad_resid1.astype(BF16)
    grad_output_bias = column_sum(grad_attn)
    part_output = scatter_all(over_rows(context_low, grad_attn))
    grad_context = against(grad_attn, w_output).astype(BF16)

    grad_queries = []
    grad_pairs = []
    for i in range(CHUNKS):
        grad_query, grad_terms = attend_back(
            queries[i], grad_context[:, chunk * i : chunk * (i + 1)], pairs[i]
        )
        grad_queries.append(grad_query)
        grad_pairs.append(
            lax.psum_scatter(grad_terms, "cp", scatter_dimension=0, tiled=True)
        )
    grad_query_low = jnp.concatenate(grad_queries, axis=1)
    grad_pair_low = jnp.concatenate(grad_pairs, axis=1)
    grad_proj = jnp.concatenate([grad_query_low, grad_pair_low], axis=1)
    part_proj = scatter_all(over_rows(local_tokens, grad_proj))
    grad_tokens = grad_resid1 + against(grad_proj, w_proj)
    proj_sums = column_sum(grad_proj)
    _, grad_value_bias = unmixed(proj_sums[None, width:])

    small_grads = (
        proj_sums[:width],
        grad_value_bias[0],
        grad_output_bias,
        grad_gain1,
        grad_shift1,
        grad_up_bias,
        grad_down_bias,
        grad_gain2,
        grad_shift2,
    )
    flat = jnp.concatenate(small_grads + (jnp.sum(grad_tokens * grad_tokens)[None],))
    sums = lax.psum(flat, ("rep", "cp"))
    place = lax.axis_index("cp")
    reduced = []
    at = 0
    for vector, shard in zip(small_grads, small):
        own = lax.dynamic_slice_in_dim(
            sums, at + place * shard.shape[0], shard.shape[0], 0
        )
        reduced.append(own)
        at += vector.shape[0]
    entries = lax.axis_size("rep") * lax.axis_size("cp") * row_count * width
    rms_values = jnp.sqrt(sums[at:] / entries)

    full_down = lax.all_gather(part_down, "rep", axis=0, tiled=True).astype(F32)
    full_wide = lax.all_gather(
        jnp.concatenate([part_output, part_up], axis=1), "rep", axis=0, tiled=True
    ).astype(F32)
    full_proj = lax.all_gather(part_proj, "rep", axis=0, tiled=True).astype(F32)
    grad_key_weight, grad_value_weight = unmixed(full_proj[:, width:])
    return (
        layer_out[None],
        grad_tokens[None],
        full_proj[:, :width],
        reduced[0],
        grad_key_weight,
        grad_value_weight,
        reduced[1],
        full_wide[:, :width],
        reduced[2],
        reduced[3],
        reduced[4],
        full_wide[:, width:],
        reduced[5],
        full_down,
        reduced[6],
        reduced[7],
        reduced[8],
        rms_values,
    )


def solution(mesh):
    rows = P("cp", None)
    vector = P("cp")
    whole = P("rep", "cp", None)
    params = (
        rows,
        vector,
        rows,
        rows,
        vector,
        rows,
        vector,
        vector,
        vector,
        rows,
        vector,
        rows,
        vector,
        vector,
        vector,
    )
    return jax.shard_map(
        on_device,
        mesh=mesh,
        in_specs=(whole,) + params + (whole,),
        out_specs=(whole, whole) + params + (P(),),
        check_vma=False,
    )
```

time: 780 us -> 897 us (1.15)
  waiting for transfers between devices: 443 us -> 657 us
  matrix products: 103 us -> 39.7 us
  Pallas kernels: 0 us -> 52.9 us
  blocking collectives: 119 us -> 87.6 us
  local copies, waits for them, and re-layouts: 59.7 us -> 28.7 us
  other arithmetic: 34 us -> 9.84 us
    reduce_scatter x4 -> x7, waiting for transfers between devices: 208 us -> 417 us  [the longest x4 349 us: scatter_all(): lax.psum_scatter(values.astype(BF16), BOTH, scatter_dimension=0, tiled=True)]
    all_gather x8 -> x6, waiting for transfers between devices: 150 us -> 239 us  [the longest x3 168 us: gather_all(): return lax.all_gather(own_rows(shard), BOTH, axis=0, tiled=True)]
    unnamed x19 -> x13, waiting for transfers between devices: 84.9 us -> 1.38 us
    dot_general x46 -> x13, matrix products: 103 us -> 39.7 us  [the longest x5 15.9 us: matmul(): return jnp.dot(left, right, preferred_element_type=F32)]
    unnamed x2 -> x0, blocking collectives: 57.6 us -> none
    pallas_call x0 -> x6, Pallas kernels: none -> 52.9 us  [the longest x3 33.8 us: attend_back(): pl.pallas_call(backward_kernel, grid=(width // PAIR,), in_specs=[column_b...]
    all_gather x1 -> x4, blocking collectives: 12.8 us -> 49.5 us  [the longest x1 15.8 us: on_device(): lax.all_gather(jnp.concatenate(small)[None], 'cp', axis=0, tiled=True)]
    unnamed x158 -> x91, local copies, waits for them, and re-layouts: 34.4 us -> 12.5 us
  transfers between devices with their start and end apart: 16 -> 13, of which waited for: 13 -> 12; matrix products, arithmetic and copies ran while one was open for 15% -> 6% of each run, Pallas kernels for 0% -> 5%
where the time goes in v1:
time: 897 us; the launch traced here: 894 us
  waiting for transfers between devices  657 us (73%)
  blocking collectives  87.6 us (10%)
  Pallas kernels  52.9 us (6%)
  matrix products  39.7 us (4%)
  local copies, waits for them, and re-layouts  28.7 us (3%)
  between operations  16.6 us (2%)
  other arithmetic  9.84 us (1%)
    reduce_scatter x4, waiting for transfers between devices, scatter_all(): lax.psum_scatter(values.astype(BF16), BOTH, scatter_dimension=0, tiled=True)  349 us
    all_gather x3, waiting for transfers between devices, gather_all(): return lax.all_gather(own_rows(shard), BOTH, axis=0, tiled=True)  168 us
    all_gather x3, waiting for transfers between devices, on_device(): lax.all_gather(pair_rows[:, 2 * chunk * i:2 * chunk * (i + 1)], 'cp', axi...  70.5 us
    reduce_scatter x3, waiting for transfers between devices, on_device(): lax.psum_scatter(grad_terms, 'cp', scatter_dimension=0, tiled=True)  68.9 us
    psum x1, blocking collectives, on_device(): sums = lax.psum(flat, ('rep', 'cp'))  38.1 us
    pallas_call x3, Pallas kernels, attend_back(): pl.pallas_call(backward_kernel, grid=(width // PAIR,), in_specs=[column_b...  33.8 us
    pallas_call x3, Pallas kernels, attend(): pl.pallas_call(forward_kernel, grid=(width // PAIR,), in_specs=[column_bl...  19.1 us
  transfers between devices with their start and end apart: 13, of which 12 were waited for; matrix products, arithmetic and copies ran while one was open for 6% of the time, Pallas kernels for 5%

profile of v1, /device:TPU:0, one launch (start us, length us, event | category | flops | bytes accessed | tf_op | source)
XLA Modules:
  0.0 893.6 jit_solution(4847740328333591165)
XLA Ops:
  7.4 1.2 stack_reshape.8
  8.6 1.1 stack_reshape.7
  10.3 1.4 fusion.28
  12.0 15.8 %all-gather.1 = bf16[8,1,1152]{2,1,0:T(2,128)(2,1)S(1)} all-gather(bf16[1,1,1152]{2,1,0:T(2,128)(2,1)S(1)} %reshape.193), channel_id=2, replica_groups=mesh['rep'=4,'cp'=8] {'cp'}, dimensions={0}, use_global_device_ids=true | all-gather | bytes 20736 | tf_op jit(solution)/shard_map/all_gather | solution.py:198
  28.0 46.6 %all-gather.9.cloned.1.call-done = bf16[768,2304]{1,0:T(8,128)(2,1)} async-done(((bf16[24,2304]{1,0:T(8,128)(2,1)}), bf16[768,2304]{1,0:T(8,128)(2,1)}) %all-gather.9.cloned.1.call-update) | async-done | bytes 3538960 | tf_op jit(solution)/shard_map/all_gather | solution.py:155
  74.6 2.4 fusion.9
  77.1 0.9 fusion.37
  78.0 0.7 all-gather.13.cloned.1.call-update
  79.4 0.7 fusion.27
  80.2 0.7 constant_dynamic-slice_fusion
  81.7 1.8 fusion.18
  83.4 0.7 fusion.39
  84.2 21.9 %all-gather.15.cloned.1.call-done.pair_ref = bf16[2048,512]{1,0:T(8,128)(2,1)} async-done(((bf16[256,512]{1,0:T(8,128)(2,1)}), bf16[2048,512]{1,0:T(8,128)(2,1)}) %all-gather.15.cloned.1.call-update) | async-done | bytes 2097168 | tf_op jit(solution)/shard_map/all_gather | solution.py:211
  106.1 6.4 shard_map.306
  112.5 24.4 %all-gather.13.cloned.1.call-done.pair_ref = bf16[2048,512]{1,0:T(8,128)(2,1)} async-done(((bf16[256,512]{1,0:T(8,128)(2,1)}), bf16[2048,512]{1,0:T(8,128)(2,1)}) %all-gather.13.cloned.1.call-update) | async-done | bytes 2097168 | tf_op jit(solution)/shard_map/all_gather | solution.py:211
  136.8 6.4 shard_map.305
  143.2 24.2 %all-gather.11.cloned.1.call-done.pair_ref = bf16[2048,512]{1,0:T(8,128)(2,1)} async-done(((bf16[256,512]{1,0:T(8,128)(2,1)}), bf16[2048,512]{1,0:T(8,128)(2,1)}) %all-gather.11.cloned.1.call-update) | async-done | bytes 2097168 | tf_op jit(solution)/shard_map/all_gather | solution.py:211
  167.4 6.4 shard_map.304
  173.8 64.1 %all-gather.17.cloned.1.call-done = bf16[768,3840]{1,0:T(8,128)(2,1)} async-done(((bf16[24,3840]{1,0:T(8,128)(2,1)}), bf16[768,3840]{1,0:T(8,128)(2,1)}) %all-gather.17.cloned.1.call-update) | async-done | bytes 5898256 | tf_op jit(solution)/shard_map/all_gather | solution.py:155
  237.9 2.0 fusion.41
  240.1 5.7 multiply_convert_fusion
  245.9 57.5 %all-gather.19.cloned.1.call-done = bf16[3072,768]{1,0:T(8,128)(2,1)} async-done(((bf16[96,768]{1,0:T(8,128)(2,1)}), bf16[3072,768]{1,0:T(8,128)(2,1)}) %all-gather.19.cloned.1.call-update) | async-done | bytes 4718608 | tf_op jit(solution)/shard_map/all_gather | solution.py:155
  303.4 4.0 fusion.42
  308.0 1.2 fusion.36
  309.2 0.7 convert_reduce_fusion.2
  310.2 3.4 convert_reduce_fusion
  313.6 2.2 multiply_reduce_fusion.1
  316.2 0.8 copy-done.4
  317.0 0.7 convert_reduce_fusion.3
  318.3 0.7 fusion.38
  319.0 11.1 %shard_map.307 = (bf16[256,256]{1,0:T(8,128)(2,1)}, bf16[2048,512]{1,0:T(8,128)(2,1)}) custom-call(bf16[256,256]{1,0:T(8,128)(2,1)} %get-tuple-element.90.query_ref, bf16[256,256]{1,0:T(8,128)(2,1)} %get-tuple-element.89.grad_ref, bf16[2048,512]{1,0:T(8,128)(2,1)} %all-gather.11.cloned.1.call-done.pair_ref), custom_call_target="tpu_custom_call" | custom-call | tf_op jit(solution)/shard_map/pallas_call | solution.py:119
  330.2 11.1 %shard_map.308 = (bf16[256,256]{1,0:T(8,128)(2,1)}, bf16[2048,512]{1,0:T(8,128)(2,1)}) custom-call(bf16[256,256]{1,0:T(8,128)(2,1)} %get-tuple-element.92.query_ref, bf16[256,256]{1,0:T(8,128)(2,1)} %get-tuple-element.88.grad_ref, bf16[2048,512]{1,0:T(8,128)(2,1)} %all-gather.13.cloned.1.call-done.pair_ref), custom_call_target="tpu_custom_call" | custom-call | tf_op jit(solution)/shard_map/pallas_call | solution.py:119
  341.4 11.6 %shard_map.309 = (bf16[256,256]{1,0:T(8,128)(2,1)}, bf16[2048,512]{1,0:T(8,128)(2,1)}) custom-call(bf16[256,256]{1,0:T(8,128)(2,1)} %get-tuple-element.91.query_ref, bf16[256,256]{1,0:T(8,128)(2,1)} %get-tuple-element.87.grad_ref, bf16[2048,512]{1,0:T(8,128)(2,1)} %all-gather.15.cloned.1.call-done.pair_ref), custom_call_target="tpu_custom_call" | custom-call | tf_op jit(solution)/shard_map/pallas_call | solution.py:119
  353.0 1.5 convolution_convert_fusion.3
  354.6 5.1 convolution_convert_fusion.1
  359.9 3.6 convolution_convert_fusion
  363.6 0.8 copy-done.13
  365.1 0.7 constant_dynamic-update-slice_fusion.4
  365.7 0.7 constant_dynamic-update-slice_fusion.3
  366.4 1.7 constant_dynamic-update-slice_fusion.2
  368.1 33.6 %reduce-scatter.12.cloned.1.call-done = bf16[256,512]{1,0:T(8,128)(2,1)} async-done(((bf16[2048,512]{1,0:T(8,128)(2,1)}), bf16[256,512]{1,0:T(8,128)(2,1)}) %reduce-scatter.12.cloned.1.call-update) | async-done | bytes 262160 | tf_op jit(solution)/shard_map/reduce_scatter | solution.py:259
  401.6 1.7 constant_dynamic-update-slice_fusion.1
  403.3 35.3 %reduce-scatter.14.cloned.1.call-done = bf16[256,512]{1,0:T(8,128)(2,1)} async-done(((bf16[2048,512]{1,0:T(8,128)(2,1)}), bf16[256,512]{1,0:T(8,128)(2,1)}) %reduce-scatter.14.cloned.1.call-update) | async-done | bytes 262160 | tf_op jit(solution)/shard_map/reduce_scatter | solution.py:259
  438.6 1.7 constant_dynamic-update-slice_fusion
  440.3 2.5 fusion
  442.8 4.0 copy.56
  446.9 1.0 copy-done.3
  448.0 1.5 convert_reduce_fusion.1
  449.7 5.0 multiply_reduce_fusion
  455.3 38.1 %psum.7 = f32[9217]{0:T(1024)S(1)} all-reduce(f32[9217]{0:T(1024)S(1)} %constant_dynamic-update-slice_fusion.8), channel_id=1, replica_groups=mesh['rep'=4,'cp'=8] {'rep','cp'}, use_global_device_ids=true, to_apply=%region_21.0 | all-reduce | flops 9217 | bytes 73736 | tf_op jit(solution)/shard_map/psum | solution.py:281
  495.9 44.0 %reduce-scatter.16.cloned.1.call-done = bf16[24,768]{1,0:T(8,128)(2,1)} async-done(((bf16[768,768]{1,0:T(8,128)(2,1)}), bf16[24,768]{1,0:T(8,128)(2,1)}) %reduce-scatter.16.cloned.1.call-update) | async-done | bytes 36880 | tf_op jit(solution)/shard_map/reduce_scatter | solution.py:159
  540.0 112.0 %reduce-scatter.18.cloned.1.call-done = bf16[24,3072]{1,0:T(8,128)(2,1)} async-done(((bf16[768,3072]{1,0:T(8,128)(2,1)}), bf16[24,3072]{1,0:T(8,128)(2,1)}) %reduce-scatter.18.cloned.1.call-update) | async-done | bytes 147472 | tf_op jit(solution)/shard_map/reduce_scatter | solution.py:159
  652.0 0.9 pad_maximum_fusion.2
  652.9 12.2 %all_gather.38 = bf16[96,3840]{1,0:T(8,128)(2,1)S(1)} all-gather(bf16[24,3840]{1,0:T(8,128)(2,1)S(1)} %pad_maximum_fusion.2), channel_id=1, replica_groups=mesh['rep'=4,'cp'=8] {'rep'}, dimensions={0}, use_global_device_ids=true | all-gather | bytes 921600 | tf_op jit(solution)/shard_map/all_gather | solution.py:295
  665.1 0.7 slice.157
  665.8 1.1 slice.158
  666.9 96.9 %reduce-scatter.20.cloned.1.call-done = bf16[96,768]{1,0:T(8,128)(2,1)} async-done(((bf16[3072,768]{1,0:T(8,128)(2,1)}), bf16[96,768]{1,0:T(8,128)(2,1)}) %reduce-scatter.20.cloned.1.call-update) | async-done | bytes 147472 | tf_op jit(solution)/shard_map/reduce_scatter | solution.py:159
  763.9 11.1 %all_gather.39 = bf16[384,768]{1,0:T(8,128)(2,1)S(1)} all-gather(bf16[96,768]{1,0:T(8,128)(2,1)} %reduce-scatter.20.cloned.1.call-done), channel_id=1, replica_groups=mesh['rep'=4,'cp'=8] {'rep'}, dimensions={0}, use_global_device_ids=true | all-gather | bytes 737280 | tf_op jit(solution)/shard_map/all_gather | solution.py:294
  774.9 1.1 convert_element_type.196
  776.0 95.6 %reduce-scatter.22.cloned.1.call-done = bf16[24,2304]{1,0:T(8,128)(2,1)} async-done(((bf16[768,2304]{1,0:T(8,128)(2,1)}), bf16[24,2304]{1,0:T(8,128)(2,1)}) %reduce-scatter.22.cloned.1.call-update) | async-done | bytes 110608 | tf_op jit(solution)/shard_map/reduce_scatter | solution.py:159
  871.6 10.5 %all_gather.37 = bf16[96,2304]{1,0:T(8,128)(2,1)S(1)} all-gather(bf16[24,2304]{1,0:T(8,128)(2,1)} %reduce-scatter.22.cloned.1.call-done), channel_id=1, replica_groups=mesh['rep'=4,'cp'=8] {'rep'}, dimensions={0}, use_global_device_ids=true | all-gather | bytes 552960 | tf_op jit(solution)/shard_map/all_gather | solution.py:298
  882.1 0.7 slice.150
  883.3 1.6 slice_reduce_fusion
  884.8 0.9 copy_bitcast_fusion
  (151 shorter events, 8.7 us)
Async XLA Ops:
  7.2 73.0 %copy-start = (bf16[384,768]{1,0:T(8,128)(2,1)S(1)}, bf16[384,768]{1,0:T(8,128)(2,1)}, u32[]{:S(2)}) copy-start(bf16[384,768]{1,0:T(8,128)(2,1)} %param.29) | copy-start | bytes 1769476
  7.2 4.6 copy-start.25
  7.2 4.6 copy-start.26
  7.2 4.6 copy-start.27
  7.2 4.6 copy-start.28
  7.3 4.6 copy-start.29
  7.3 4.6 copy-start.24
  7.3 4.6 copy-start.30
  7.3 4.6 copy-start.31
  7.3 4.6 copy-start.32
  7.3 67.3 %copy-start.8 = (bf16[1,256,768]{2,1,0:T(8,128)(2,1)S(1)}, bf16[1,256,768]{2,1,0:T(8,128)(2,1)}, u32[]{:S(2)}) copy-start(bf16[1,256,768]{2,1,0:T(8,128)(2,1)} %param.17) | copy-start | bytes 1179652
  7.3 67.3 %all-gather.9.cloned.1.call-start = ((), (), s32[]{:S(2)}) async-start(), calls=%async_computation.7 | async-start | bytes 3649536 | tf_op jit(solution)/shard_map/all_gather | solution.py:155
  11.8 94.3 %all-gather.15.cloned.1.call-start = ((), (), s32[]{:S(2)}) async-start(), calls=%async_computation.10 | async-start | bytes 2359296 | tf_op jit(solution)/shard_map/all_gather | solution.py:211
  28.0 51.4 %copy-start.7 = (bf16[96,3072]{1,0:T(8,128)(2,1)S(1)}, bf16[96,3072]{1,0:T(8,128)(2,1)}, u32[]{:S(2)}) copy-start(bf16[96,3072]{1,0:T(8,128)(2,1)} %param.27) | copy-start | bytes 1769476
  28.0 51.4 %copy-start.9 = (bf16[96,768]{1,0:T(8,128)(2,1)S(1)}, bf16[96,768]{1,0:T(8,128)(2,1)}, u32[]{:S(2)}) copy-start(bf16[96,768]{1,0:T(8,128)(2,1)} %param.23) | copy-start | bytes 442372
  78.0 58.8 %all-gather.13.cloned.1.call-start = ((), (), s32[]{:S(2)}) async-start(), calls=%async_computation.9 | async-start | bytes 2359296 | tf_op jit(solution)/shard_map/all_gather | solution.py:211
  78.7 88.7 %all-gather.11.cloned.1.call-start = ((), (), s32[]{:S(2)}) async-start(), calls=%async_computation.8 | async-start | bytes 2359296 | tf_op jit(solution)/shard_map/all_gather | solution.py:211
  79.3 158.6 %all-gather.17.cloned.1.call-start = ((), (), s32[]{:S(2)}) async-start(), calls=%async_computation.11 | async-start | bytes 6082560 | tf_op jit(solution)/shard_map/all_gather | solution.py:155
  80.1 223.3 %all-gather.19.cloned.1.call-start = ((), (), s32[]{:S(2)}) async-start(), calls=%async_computation.12 | async-start | bytes 4866048 | tf_op jit(solution)/shard_map/all_gather | solution.py:155
  80.9 285.5 %reduce-scatter.10.cloned.1.call-start = ((), (), s32[]{:S(2)}) async-start(), calls=%async_computation.13 | async-start | bytes 2359296 | tf_op jit(solution)/shard_map/reduce_scatter | solution.py:259
  112.5 125.4 %copy-start.10 = (bf16[256,256]{1,0:T(8,128)(2,1)S(1)}, bf16[256,256]{1,0:T(8,128)(2,1)}, u32[]{:S(2)}) copy-start(bf16[256,256]{1,0:T(8,128)(2,1)} %shard_map.306) | copy-start | bytes 393220
  240.1 75.7 %copy-start.18 = (f32[256]{0:T(256)}, f32[256]{0:T(256)S(1)}, u32[]{:S(2)}) copy-start(f32[256]{0:T(256)S(1)} %fusion.29) | copy-start | bytes 3076
  303.4 4.2 copy-start.2
  303.4 6.6 copy-start.34
  307.6 2.6 copy-start.33
  309.2 4.4 slice-start
  310.2 3.4 slice-start.1
  313.6 4.2 copy-start.6
  316.1 0.9 copy-start.4
  316.1 14.0 %copy-start.22 = (f32[256]{0:T(256)}, f32[256]{0:T(256)S(1)}, u32[]{:S(2)}) copy-start(f32[256]{0:T(256)S(1)} %negate_multiply_fusion) | copy-start | bytes 3076
  330.1 71.5 %reduce-scatter.12.cloned.1.call-start = ((), (), s32[]{:S(2)}) async-start(), calls=%async_computation.14 | async-start | bytes 2359296 | tf_op jit(solution)/shard_map/reduce_scatter | solution.py:259
  341.3 11.7 %copy-start.11 = (bf16[256,256]{1,0:T(8,128)(2,1)S(1)}, bf16[256,256]{1,0:T(8,128)(2,1)}, u32[]{:S(2)}) copy-start(bf16[256,256]{1,0:T(8,128)(2,1)} %shard_map.305) | copy-start | bytes 393220
  341.3 11.7 %copy-start.12 = (bf16[256,256]{1,0:T(8,128)(2,1)S(1)}, bf16[256,256]{1,0:T(8,128)(2,1)}, u32[]{:S(2)}) copy-start(bf16[256,256]{1,0:T(8,128)(2,1)} %shard_map.304) | copy-start | bytes 393220
  341.3 97.3 %reduce-scatter.14.cloned.1.call-start = ((), (), s32[]{:S(2)}) async-start(), calls=%async_computation.15 | async-start | bytes 2359296 | tf_op jit(solution)/shard_map/reduce_scatter | solution.py:259
  353.0 187.0 %reduce-scatter.16.cloned.1.call-start = ((), (), s32[]{:S(2)}) async-start(), calls=%async_computation.16 | async-start | bytes 1216512 | tf_op jit(solution)/shard_map/reduce_scatter | solution.py:159
  354.6 297.4 %reduce-scatter.18.cloned.1.call-start = ((), (), s32[]{:S(2)}) async-start(), calls=%async_computation.17 | async-start | bytes 4866048 | tf_op jit(solution)/shard_map/reduce_scatter | solution.py:159
  359.8 404.0 %reduce-scatter.20.cloned.1.call-start = ((), (), s32[]{:S(2)}) async-start(), calls=%async_computation.18 | async-start | bytes 4866048 | tf_op jit(solution)/shard_map/reduce_scatter | solution.py:159
  363.5 0.9 copy-start.13
  363.5 1.6 copy-start.14
  363.5 2.2 copy-start.15
  363.5 508.1 %reduce-scatter.22.cloned.1.call-start = ((), (), s32[]{:S(2)}) async-start(), calls=%async_computation.19 | async-start | bytes 3649536 | tf_op jit(solution)/shard_map/reduce_scatter | solution.py:159
  446.8 1.1 copy-start.3
  446.8 2.7 copy-start.17
  446.8 2.8 copy-start.21
  446.8 2.8 copy-start.20
  446.8 2.8 copy-start.19
  446.8 2.8 copy-start.16
  446.8 2.9 copy-start.5
  446.8 2.9 copy-start.23
  774.9 110.8 %copy-start.1 = (bf16[384,768]{1,0:T(8,128)(2,1)S(1)}, bf16[384,768]{1,0:T(8,128)(2,1)}, u32[]{:S(2)}) copy-start(bf16[384,768]{1,0:T(8,128)(2,1)} %param.29) | copy-start | bytes 1769476
Sparse Core Ops, SparseCore 0:
  11.9 62.6 all-gather.8
  78.1 27.9 all-gather.14
  108.3 28.5 all-gather.12
  138.9 28.5 all-gather.10
  170.8 67.0 all-gather.16
  241.2 62.1 all-gather.18
  330.3 34.2 reduce-scatter.9
  366.8 34.7 reduce-scatter.11
  403.9 34.6 reduce-scatter.13
  444.1 95.7 reduce-scatter.15
  545.4 106.4 reduce-scatter.17
  657.3 106.4 reduce-scatter.19
  769.3 102.2 reduce-scatter.21

commit v2 on v1

--- a/solution.py
+++ b/solution.py
@@ -13,7 +13,6 @@
 EPSILON = 1e-12
 BF16 = jnp.bfloat16
 F32 = jnp.float32
-BOTH = ("cp", "rep")
 
 
 def normalize(values, norm_gain, norm_shift):
@@ -146,17 +145,12 @@
     return parts[:, :, 0].reshape(rows, width // 2), parts[:, :, 1].reshape(rows, width // 2)
 
 
-def own_rows(shard):
-    share = shard.shape[0] // lax.axis_size("rep")
-    return lax.dynamic_slice_in_dim(shard, lax.axis_index("rep") * share, share, 0)
-
-
 def gather_all(shard):
-    return lax.all_gather(own_rows(shard), BOTH, axis=0, tiled=True)
+    return lax.all_gather(shard, "cp", axis=0, tiled=True)
 
 
 def scatter_all(values):
-    return lax.psum_scatter(values.astype(BF16), BOTH, scatter_dimension=0, tiled=True)
+    return lax.psum_scatter(values.astype(BF16), "cp", scatter_dimension=0, tiled=True)
 
 
 def on_device(
@@ -291,11 +285,10 @@
     entries = lax.axis_size("rep") * lax.axis_size("cp") * row_count * width
     rms_values = jnp.sqrt(sums[at:] / entries)
 
-    full_down = lax.all_gather(part_down, "rep", axis=0, tiled=True).astype(F32)
-    full_wide = lax.all_gather(
-        jnp.concatenate([part_output, part_up], axis=1), "rep", axis=0, tiled=True
-    ).astype(F32)
-    full_proj = lax.all_gather(part_proj, "rep", axis=0, tiled=True).astype(F32)
+    full_down, full_up, full_output, full_proj = [
+        part.astype(F32)
+        for part in lax.psum((part_down, part_up, part_output, part_proj), "rep")
+    ]
     grad_key_weight, grad_value_weight = unmixed(full_proj[:, width:])
     return (
         layer_out[None],
@@ -305,11 +298,11 @@
         grad_key_weight,
         grad_value_weight,
         reduced[1],
-        full_wide[:, :width],
+        full_output,
         reduced[2],
         reduced[3],
         reduced[4],
-        full_wide[:, width:],
+        full_up,
         reduced[5],
         full_down,
         reduced[6],

time: 897 us -> 684 us (0.76)
  waiting for transfers between devices: 657 us -> 475 us
  blocking collectives: 87.6 us -> 54.4 us
    reduce_scatter x4 -> x3, waiting for transfers between devices: 349 us -> 143 us  [scatter_all(): lax.psum_scatter(values.astype(BF16), 'cp', scatter_dimension=0, tiled=True)]
    all_gather x3, waiting for transfers between devices: 168 us -> 128 us  [gather_all(): return lax.all_gather(shard, 'cp', axis=0, tiled=True)]
    all_gather x3 -> x0, blocking collectives: 33.7 us -> none  [the longest x1 12.2 us: on_device(): lax.all_gather(jnp.concatenate([part_output, part_up], axis=1), 'rep', ax...]
    unnamed x13 -> x15, waiting for transfers between devices: 1.38 us -> 30.2 us
    psum x0 -> x1, waiting for transfers between devices: none -> 22.6 us  [on_device(): lax.psum((part_down, part_up, part_output, part_proj), 'rep')]
    reduce_scatter x3, waiting for transfers between devices: 68.9 us -> 80.1 us  [on_device(): lax.psum_scatter(grad_terms, 'cp', scatter_dimension=0, tiled=True)]
  transfers between devices with their start and end apart: 13 -> 14, of which waited for: 12 -> 14; matrix products, arithmetic and copies ran while one was open for 6% -> 6% of each run, Pallas kernels for 5% -> 6%
where the time goes in v2:
time: 684 us; the launch traced here: 681 us
  waiting for transfers between devices  475 us (69%)
  blocking collectives  54.4 us (8%)
  Pallas kernels  52.7 us (8%)
  matrix products  38.3 us (6%)
  local copies, waits for them, and re-layouts  31.8 us (5%)
  between operations  16.9 us (2%)
  other arithmetic  11.2 us (2%)
    reduce_scatter x3, waiting for transfers between devices, scatter_all(): lax.psum_scatter(values.astype(BF16), 'cp', scatter_dimension=0, tiled=True)  143 us
    all_gather x3, waiting for transfers between devices, gather_all(): return lax.all_gather(shard, 'cp', axis=0, tiled=True)  128 us
    reduce_scatter x3, waiting for transfers between devices, on_device(): lax.psum_scatter(grad_terms, 'cp', scatter_dimension=0, tiled=True)  80.1 us
    all_gather x3, waiting for transfers between devices, on_device(): lax.all_gather(pair_rows[:, 2 * chunk * i:2 * chunk * (i + 1)], 'cp', axi...  70.5 us
    psum x1, blocking collectives, on_device(): sums = lax.psum(flat, ('rep', 'cp'))  38.6 us
    pallas_call x3, Pallas kernels, attend_back(): pl.pallas_call(backward_kernel, grid=(width // PAIR,), in_specs=[column_b...  33.6 us
    unnamed x15, waiting for transfers between devices  30.2 us
    psum x1, waiting for transfers between devices, on_device(): lax.psum((part_down, part_up, part_output, part_proj), 'rep')  22.6 us
  transfers between devices with their start and end apart: 14, of which 14 were waited for; matrix products, arithmetic and copies ran while one was open for 6% of the time, Pallas kernels for 6%

profile of v2, /device:TPU:0, one launch (start us, length us, event | category | flops | bytes accessed | tf_op | source)
XLA Modules:
  0.0 680.9 jit_solution(2952259588871588592)
XLA Ops:
  7.3 1.2 stack_reshape.8
  8.5 1.1 stack_reshape.7
  10.2 1.7 pad_maximum_fusion.1
  12.2 15.8 %all-gather.1 = bf16[8,1,1152]{2,1,0:T(2,128)(2,1)S(1)} all-gather(bf16[1,1,1152]{2,1,0:T(2,128)(2,1)S(1)} %reshape.193), channel_id=2, replica_groups=mesh['rep'=4,'cp'=8] {'cp'}, dimensions={0}, use_global_device_ids=true | all-gather | bytes 20736 | tf_op jit(solution)/shard_map/all_gather | solution.py:192
  28.3 28.1 %all-gather.9.cloned.1.call-done = bf16[768,2304]{1,0:T(8,128)(2,1)} async-done(((bf16[96,2304]{1,0:T(8,128)(2,1)}), bf16[768,2304]{1,0:T(8,128)(2,1)}) %all-gather.9.cloned.1.call-update) | async-done | bytes 3538960 | tf_op jit(solution)/shard_map/all_gather | solution.py:149
  56.4 2.4 fusion.9
  58.8 0.9 fusion.36
  59.8 0.7 all-gather.13.cloned.1.call-update
  61.1 0.9 pad_maximum_fusion
  63.4 1.8 fusion.18
  65.2 0.7 fusion.38
  65.9 21.9 %all-gather.15.cloned.1.call-done.pair_ref = bf16[2048,512]{1,0:T(8,128)(2,1)} async-done(((bf16[256,512]{1,0:T(8,128)(2,1)}), bf16[2048,512]{1,0:T(8,128)(2,1)}) %all-gather.15.cloned.1.call-update) | async-done | bytes 2097168 | tf_op jit(solution)/shard_map/all_gather | solution.py:205
  87.9 6.4 shard_map.306
  94.2 24.4 %all-gather.13.cloned.1.call-done.pair_ref = bf16[2048,512]{1,0:T(8,128)(2,1)} async-done(((bf16[256,512]{1,0:T(8,128)(2,1)}), bf16[2048,512]{1,0:T(8,128)(2,1)}) %all-gather.13.cloned.1.call-update) | async-done | bytes 2097168 | tf_op jit(solution)/shard_map/all_gather | solution.py:205
  118.6 6.4 shard_map.305
  125.0 24.2 %all-gather.11.cloned.1.call-done.pair_ref = bf16[2048,512]{1,0:T(8,128)(2,1)} async-done(((bf16[256,512]{1,0:T(8,128)(2,1)}), bf16[2048,512]{1,0:T(8,128)(2,1)}) %all-gather.11.cloned.1.call-update) | async-done | bytes 2097168 | tf_op jit(solution)/shard_map/all_gather | solution.py:205
  149.2 6.4 shard_map.304
  155.6 56.6 %all-gather.17.cloned.1.call-done = bf16[768,3840]{1,0:T(8,128)(2,1)} async-done(((bf16[96,3840]{1,0:T(8,128)(2,1)}), bf16[768,3840]{1,0:T(8,128)(2,1)}) %all-gather.17.cloned.1.call-update) | async-done | bytes 5898256 | tf_op jit(solution)/shard_map/all_gather | solution.py:149
  212.2 2.0 fusion.40
  214.4 5.8 multiply_convert_fusion
  220.2 43.4 %all-gather.19.cloned.1.call-done = bf16[3072,768]{1,0:T(8,128)(2,1)} async-done(((bf16[384,768]{1,0:T(8,128)(2,1)}), bf16[3072,768]{1,0:T(8,128)(2,1)}) %all-gather.19.cloned.1.call-update) | async-done | bytes 4718608 | tf_op jit(solution)/shard_map/all_gather | solution.py:149
  263.6 4.0 fusion.41
  268.2 1.2 fusion.34
  269.4 0.7 convert_reduce_fusion.2
  270.4 3.4 convert_reduce_fusion
  273.8 2.2 multiply_reduce_fusion.1
  276.4 0.8 copy-done.6
  277.3 0.7 convert_reduce_fusion.3
  278.5 0.8 fusion.37
  279.3 11.1 %shard_map.307 = (bf16[256,256]{1,0:T(8,128)(2,1)}, bf16[2048,512]{1,0:T(8,128)(2,1)}) custom-call(bf16[256,256]{1,0:T(8,128)(2,1)} %get-tuple-element.112.query_ref, bf16[256,256]{1,0:T(8,128)(2,1)} %get-tuple-element.111.grad_ref, bf16[2048,512]{1,0:T(8,128)(2,1)} %all-gather.11.cloned.1.call-done.pair_ref), custom_call_target="tpu_custom_call" | custom-call | tf_op jit(solution)/shard_map/pallas_call | solution.py:118
  290.4 11.1 %shard_map.308 = (bf16[256,256]{1,0:T(8,128)(2,1)}, bf16[2048,512]{1,0:T(8,128)(2,1)}) custom-call(bf16[256,256]{1,0:T(8,128)(2,1)} %get-tuple-element.114.query_ref, bf16[256,256]{1,0:T(8,128)(2,1)} %get-tuple-element.110.grad_ref, bf16[2048,512]{1,0:T(8,128)(2,1)} %all-gather.13.cloned.1.call-done.pair_ref), custom_call_target="tpu_custom_call" | custom-call | tf_op jit(solution)/shard_map/pallas_call | solution.py:118
  301.6 11.4 %shard_map.309 = (bf16[256,256]{1,0:T(8,128)(2,1)}, bf16[2048,512]{1,0:T(8,128)(2,1)}) custom-call(bf16[256,256]{1,0:T(8,128)(2,1)} %get-tuple-element.113.query_ref, bf16[256,256]{1,0:T(8,128)(2,1)} %get-tuple-element.109.grad_ref, bf16[2048,512]{1,0:T(8,128)(2,1)} %all-gather.15.cloned.1.call-done.pair_ref), custom_call_target="tpu_custom_call" | custom-call | tf_op jit(solution)/shard_map/pallas_call | solution.py:118
  314.4 1.6 constant_dynamic-update-slice_fusion.3
  316.0 9.4 %reduce-scatter.10.cloned.1.call-done = bf16[256,512]{1,0:T(8,128)(2,1)} async-done(((bf16[2048,512]{1,0:T(8,128)(2,1)}), bf16[256,512]{1,0:T(8,128)(2,1)}) %reduce-scatter.10.cloned.1.call-update) | async-done | bytes 262160 | tf_op jit(solution)/shard_map/reduce_scatter | solution.py:253
  325.3 1.7 constant_dynamic-update-slice_fusion.2
  327.0 35.4 %reduce-scatter.12.cloned.1.call-done = bf16[256,512]{1,0:T(8,128)(2,1)} async-done(((bf16[2048,512]{1,0:T(8,128)(2,1)}), bf16[256,512]{1,0:T(8,128)(2,1)}) %reduce-scatter.12.cloned.1.call-update) | async-done | bytes 262160 | tf_op jit(solution)/shard_map/reduce_scatter | solution.py:253
  362.4 1.7 constant_dynamic-update-slice_fusion.1
  364.0 35.4 %reduce-scatter.14.cloned.1.call-done = bf16[256,512]{1,0:T(8,128)(2,1)} async-done(((bf16[2048,512]{1,0:T(8,128)(2,1)}), bf16[256,512]{1,0:T(8,128)(2,1)}) %reduce-scatter.14.cloned.1.call-update) | async-done | bytes 262160 | tf_op jit(solution)/shard_map/reduce_scatter | solution.py:253
  399.4 1.7 constant_dynamic-update-slice_fusion
  401.1 2.5 fusion
  403.6 4.0 copy.56
  407.7 0.9 copy-done.17
  408.7 1.5 convolution_convert_fusion.3
  410.3 3.7 convolution_convert_fusion.1
  414.1 1.3 copy-done.5
  415.5 3.6 convolution_convert_fusion
  419.3 1.0 copy-done.3
  420.4 1.5 convert_reduce_fusion.1
  421.9 28.3 %reduce-scatter.22.cloned.1.call-done = bf16[96,2304]{1,0:T(8,128)(2,1)} async-done(((bf16[768,2304]{1,0:T(8,128)(2,1)}), bf16[96,2304]{1,0:T(8,128)(2,1)}) %reduce-scatter.22.cloned.1.call-update) | async-done | bytes 442384
  450.2 2.1 copy.57
  452.3 32.3 %reduce-scatter.16.cloned.1.call-done = bf16[96,768]{1,0:T(8,128)(2,1)} async-done(((bf16[768,768]{1,0:T(8,128)(2,1)}), bf16[96,768]{1,0:T(8,128)(2,1)}) %reduce-scatter.16.cloned.1.call-update) | async-done | bytes 147472 | tf_op jit(solution)/shard_map/reduce_scatter | solution.py:153
  484.6 55.3 %reduce-scatter.18.cloned.1.call-done = bf16[96,3072]{1,0:T(8,128)(2,1)} async-done(((bf16[768,3072]{1,0:T(8,128)(2,1)}), bf16[96,3072]{1,0:T(8,128)(2,1)}) %reduce-scatter.18.cloned.1.call-update) | async-done | bytes 589840 | tf_op jit(solution)/shard_map/reduce_scatter | solution.py:153
  539.9 55.7 %reduce-scatter.20.cloned.1.call-done = bf16[384,768]{1,0:T(8,128)(2,1)} async-done(((bf16[3072,768]{1,0:T(8,128)(2,1)}), bf16[384,768]{1,0:T(8,128)(2,1)}) %reduce-scatter.20.cloned.1.call-update) | async-done | bytes 589840 | tf_op jit(solution)/shard_map/reduce_scatter | solution.py:153
  595.7 5.0 multiply_reduce_fusion
  601.3 38.6 %psum.36 = f32[9217]{0:T(1024)S(1)} all-reduce(f32[9217]{0:T(1024)S(1)} %constant_dynamic-update-slice_fusion.8), channel_id=1, replica_groups=mesh['rep'=4,'cp'=8] {'rep','cp'}, use_global_device_ids=true, to_apply=%region_22.0 | all-reduce | flops 9217 | bytes 73736 | tf_op jit(solution)/shard_map/psum | solution.py:275
  642.5 22.6 %all-reduce.4.cloned.1.call-done = (bf16[96,2304]{0,1:T(8,128)(2,1)}, bf16[96,768]{1,0:T(8,128)(2,1)}, bf16[96,3072]{1,0:T(8,128)(2,1)}, bf16[384,768]{1,0:T(8,128)(2,1)}) async-done(((bf16[96,2304]{0,1:T(8,128)(2,1)}, bf16[96,768]{1,0:T(8,128)(2,1)}, bf16[96,3072]{1,0:T(8,128)(2,1)}, bf16[384,768]{1,0:T(8,128)(2,1)}), (bf16[96,2304]{0,1:T(8,128)(2,1)}, bf16[96,768]{1,0:T(8,128)(2,1)}, ...) | async-done | bytes 1769488 | tf_op jit(solution)/shard_map/psum | solution.py:290
  665.1 1.0 slice.142
  666.1 1.0 slice.146
  667.1 0.9 copy.53
  668.1 0.9 copy.61
  669.0 0.9 copy.62
  669.8 0.7 convert_element_type.196
  670.6 1.1 convert_element_type.198
  671.7 1.1 convert_element_type.200
  (173 shorter events, 9.7 us)
Async XLA Ops:
  7.2 4.8 copy-start.36
  7.2 4.8 copy-start.37
  7.2 4.8 copy-start.38
  7.2 4.8 copy-start.39
  7.2 4.8 copy-start.40
  7.2 4.8 copy-start.35
  7.3 4.8 copy-start.41
  7.3 4.8 copy-start.42
  7.3 4.8 copy-start.43
  7.3 49.1 %copy-start.15 = (bf16[1,256,768]{2,1,0:T(8,128)(2,1)S(1)}, bf16[1,256,768]{2,1,0:T(8,128)(2,1)}, u32[]{:S(2)}) copy-start(bf16[1,256,768]{2,1,0:T(8,128)(2,1)} %param.17) | copy-start | bytes 1179652
  7.3 49.1 %all-gather.9.cloned.1.call-start = ((), (), s32[]{:S(2)}) async-start(), calls=%async_computation.7 | async-start | bytes 3981312 | tf_op jit(solution)/shard_map/all_gather | solution.py:149
  12.0 75.9 %all-gather.15.cloned.1.call-start = ((), (), s32[]{:S(2)}) async-start(), calls=%async_computation.10 | async-start | bytes 2359296 | tf_op jit(solution)/shard_map/all_gather | solution.py:205
  28.2 32.8 %copy-start.14 = (bf16[96,3072]{1,0:T(8,128)(2,1)S(1)}, bf16[96,3072]{1,0:T(8,128)(2,1)}, u32[]{:S(2)}) copy-start(bf16[96,3072]{1,0:T(8,128)(2,1)} %param.27) | copy-start | bytes 1769476
  28.3 32.8 %copy-start.18 = (bf16[96,768]{1,0:T(8,128)(2,1)S(1)}, bf16[96,768]{1,0:T(8,128)(2,1)}, u32[]{:S(2)}) copy-start(bf16[96,768]{1,0:T(8,128)(2,1)} %param.23) | copy-start | bytes 442372
  59.7 58.9 %all-gather.13.cloned.1.call-start = ((), (), s32[]{:S(2)}) async-start(), calls=%async_computation.9 | async-start | bytes 2359296 | tf_op jit(solution)/shard_map/all_gather | solution.py:205
  60.5 88.8 %all-gather.11.cloned.1.call-start = ((), (), s32[]{:S(2)}) async-start(), calls=%async_computation.8 | async-start | bytes 2359296 | tf_op jit(solution)/shard_map/all_gather | solution.py:205
  61.0 151.1 %all-gather.17.cloned.1.call-start = ((), (), s32[]{:S(2)}) async-start(), calls=%async_computation.11 | async-start | bytes 6635520 | tf_op jit(solution)/shard_map/all_gather | solution.py:149
  62.0 201.5 %all-gather.19.cloned.1.call-start = ((), (), s32[]{:S(2)}) async-start(), calls=%async_computation.12 | async-start | bytes 5308416 | tf_op jit(solution)/shard_map/all_gather | solution.py:149
  62.6 262.7 %reduce-scatter.10.cloned.1.call-start = ((), (), s32[]{:S(2)}) async-start(), calls=%async_computation.13 | async-start | bytes 2359296 | tf_op jit(solution)/shard_map/reduce_scatter | solution.py:253
  94.2 117.9 %copy-start.20 = (bf16[256,256]{1,0:T(8,128)(2,1)S(1)}, bf16[256,256]{1,0:T(8,128)(2,1)}, u32[]{:S(2)}) copy-start(bf16[256,256]{1,0:T(8,128)(2,1)} %shard_map.306) | copy-start | bytes 393220
  214.1 61.9 %copy-start = (f32[256,768]{1,0:T(8,128)}, f32[256,768]{1,0:T(8,128)S(1)}, u32[]{:S(2)}) copy-start(f32[256,768]{1,0:T(8,128)S(1)} %get-tuple-element.132) | copy-start | bytes 2359300
  214.4 61.6 %copy-start.28 = (f32[256]{0:T(256)}, f32[256]{0:T(256)S(1)}, u32[]{:S(2)}) copy-start(f32[256]{0:T(256)S(1)} %fusion.27) | copy-start | bytes 3076
  220.2 47.4 %copy-start.4 = (bf16[256,3072]{1,0:T(8,128)(2,1)}, bf16[256,3072]{1,0:T(8,128)(2,1)S(1)}, u32[]{:S(2)}) copy-start(bf16[256,3072]{1,0:T(8,128)(2,1)S(1)} %get-tuple-element.133) | copy-start | bytes 4718596
  263.6 4.2 copy-start.2
  263.6 6.6 copy-start.45
  267.8 2.6 copy-start.44
  269.4 4.4 slice-start
  270.2 3.6 copy-start.8
  270.4 3.4 slice-start.1
  273.8 2.2 copy-start.10
  276.4 0.9 copy-start.6
  276.4 1.6 copy-start.33
  278.0 1.3 copy-start.16
  290.4 72.0 %reduce-scatter.12.cloned.1.call-start = ((), (), s32[]{:S(2)}) async-start(), calls=%async_computation.14 | async-start | bytes 2359296 | tf_op jit(solution)/shard_map/reduce_scatter | solution.py:253
  301.6 11.5 %copy-start.24 = (bf16[256,256]{1,0:T(8,128)(2,1)S(1)}, bf16[256,256]{1,0:T(8,128)(2,1)}, u32[]{:S(2)}) copy-start(bf16[256,256]{1,0:T(8,128)(2,1)} %get-tuple-element.24) | copy-start | bytes 393220
  301.6 12.2 %copy-start.25 = (bf16[256,256]{1,0:T(8,128)(2,1)S(1)}, bf16[256,256]{1,0:T(8,128)(2,1)}, u32[]{:S(2)}) copy-start(bf16[256,256]{1,0:T(8,128)(2,1)} %get-tuple-element.25) | copy-start | bytes 393220
  301.6 97.8 %reduce-scatter.14.cloned.1.call-start = ((), (), s32[]{:S(2)}) async-start(), calls=%async_computation.15 | async-start | bytes 2359296 | tf_op jit(solution)/shard_map/reduce_scatter | solution.py:253
  313.0 137.2 %reduce-scatter.22.cloned.1.call-start = ((), (), s32[]{:S(2)}) async-start(), calls=%async_computation.19 | async-start | bytes 3981312
  407.6 1.0 copy-start.17
  407.6 1.0 copy-start.21
  407.6 1.1 copy-start.22
  407.6 1.1 copy-start.23
  407.6 2.7 copy-start.1
  407.6 2.7 copy-start.11
  407.6 2.7 copy-start.29
  407.6 77.0 %reduce-scatter.16.cloned.1.call-start = ((), (), s32[]{:S(2)}) async-start(), calls=%async_computation.16 | async-start | bytes 1327104 | tf_op jit(solution)/shard_map/reduce_scatter | solution.py:153
  410.2 129.6 %reduce-scatter.18.cloned.1.call-start = ((), (), s32[]{:S(2)}) async-start(), calls=%async_computation.17 | async-start | bytes 5308416 | tf_op jit(solution)/shard_map/reduce_scatter | solution.py:153
  414.0 1.4 copy-start.5
  414.0 1.5 copy-start.9
  414.1 181.5 %reduce-scatter.20.cloned.1.call-start = ((), (), s32[]{:S(2)}) async-start(), calls=%async_computation.18 | async-start | bytes 5308416 | tf_op jit(solution)/shard_map/reduce_scatter | solution.py:153
  419.1 1.1 copy-start.3
  419.2 176.4 %copy-start.27 = (f32[768]{0:T(1024)S(1)}, f32[768]{0:T(1024)}, u32[]{:S(2)}) copy-start(f32[768]{0:T(1024)} %get-tuple-element.97) | copy-start | bytes 9220
  419.2 176.4 %copy-start.32 = (f32[768]{0:T(1024)S(1)}, f32[768]{0:T(1024)}, u32[]{:S(2)}) copy-start(f32[768]{0:T(1024)} %get-tuple-element.86) | copy-start | bytes 9220
  419.2 176.4 %copy-start.31 = (f32[768]{0:T(1024)S(1)}, f32[768]{0:T(1024)}, u32[]{:S(2)}) copy-start(f32[768]{0:T(1024)} %get-tuple-element.88) | copy-start | bytes 9220
  419.2 176.4 %copy-start.30 = (f32[3072]{0:T(1024)S(1)}, f32[3072]{0:T(1024)}, u32[]{:S(2)}) copy-start(f32[3072]{0:T(1024)} %get-tuple-element.95) | copy-start | bytes 36868
  419.2 176.5 %copy-start.26 = (f32[768]{0:T(1024)S(1)}, f32[768]{0:T(1024)}, u32[]{:S(2)}) copy-start(f32[768]{0:T(1024)} %get-tuple-element.93) | copy-start | bytes 9220
  419.2 176.5 %copy-start.7 = (f32[256,768]{1,0:T(8,128)S(1)}, f32[256,768]{1,0:T(8,128)}, u32[]{:S(2)}) copy-start(f32[256,768]{1,0:T(8,128)} %copy-done.6) | copy-start | bytes 2359300
  419.2 176.5 %copy-start.34 = (f32[256]{0:T(256)S(1)}, f32[256]{0:T(256)}, u32[]{:S(2)}) copy-start(f32[256]{0:T(256)} %copy-done.33) | copy-start | bytes 3076
  419.2 245.8 %all-reduce.4.cloned.1.call-start = ((), (), s32[]{:S(2)}) async-start(), calls=%async_computation.20 | async-start | bytes 3833856 | tf_op jit(solution)/shard_map/psum | solution.py:290
  665.1 4.8 copy-start.19
  665.1 5.5 copy-start.13
  667.1 4.5 copy-start.12
Sparse Core Ops, SparseCore 0:
  12.1 44.2 all-gather.8
  59.8 27.9 all-gather.14
  90.0 28.5 all-gather.12
  120.6 28.5 all-gather.10
  151.3 60.8 all-gather.16
  213.6 49.8 all-gather.18
  290.5 34.7 reduce-scatter.9
  327.6 34.7 reduce-scatter.11
  364.7 34.6 reduce-scatter.13
  407.8 42.3 reduce-scatter.21
  453.1 31.5 reduce-scatter.15
  486.8 53.0 reduce-scatter.17
  542.2 53.3 reduce-scatter.19
  598.9 66.1 all-reduce.3

commit v3 on v2

--- a/solution.py
+++ b/solution.py
@@ -1,3 +1,4 @@
+import functools
 import math
 
 import jax
@@ -13,6 +14,7 @@
 EPSILON = 1e-12
 BF16 = jnp.bfloat16
 F32 = jnp.float32
+MESH = pl.DeviceIdType.MESH
 
 
 def normalize(values, norm_gain, norm_shift):
@@ -153,6 +155,349 @@
     return lax.psum_scatter(values.astype(BF16), "cp", scatter_dimension=0, tiled=True)
 
 
+def places():
+    rep = lax.axis_index("rep")
+    cp = lax.axis_index("cp")
+    return rep, cp // 2, cp % 2
+
+
+def enter(rep, depth, core, reps, depths):
+    barrier = pltpu.get_barrier_semaphore()
+    peers = [(rep, 2 * depth + 1 - core)]
+    peers += [((rep + k) % reps, 2 * depth + core) for k in range(1, reps)]
+    peers += [(rep, 2 * ((depth + k) % depths) + core) for k in range(1, depths)]
+    for peer in peers:
+        pl.semaphore_signal(barrier, inc=1, device_id=peer, device_id_type=MESH)
+    pl.semaphore_wait(barrier, len(peers))
+
+
+def remote(src, dst, sends, recvs, at, peer):
+    return pltpu.make_async_remote_copy(
+        src_ref=src,
+        dst_ref=dst,
+        send_sem=sends.at[at],
+        recv_sem=recvs.at[at],
+        device_id=peer,
+        device_id_type=MESH,
+    )
+
+
+def gather_kernel(units, count, reps, depths, *refs):
+    ins = refs[:count]
+    outs = refs[count : 2 * count]
+    sends_z, recvs_z, sends_r, recvs_r, sends_c, recvs_c, local = refs[2 * count :]
+    rep, depth, core = places()
+    cp = 2 * depth + core
+    enter(rep, depth, core, reps, depths)
+    sibling = (rep, 2 * depth + 1 - core)
+    sent = []
+    copies = []
+    for at in range(count):
+        copy = pltpu.make_async_copy(ins[at], outs[at].at[depth, core], local.at[at])
+        copy.start()
+        copies.append(copy)
+    for u, (at, low, size) in enumerate(units):
+        cols = pl.ds(low, size)
+        for k in range(1, depths):
+            copy = remote(
+                ins[at].at[rep, :, cols],
+                outs[at].at[depth, core, rep, :, cols],
+                sends_z,
+                recvs_z,
+                u * (depths - 1) + k - 1,
+                (rep, 2 * ((depth + k) % depths) + core),
+            )
+            copy.start()
+            sent.append(copy)
+    for u, (at, low, size) in enumerate(units):
+        cols = pl.ds(low, size)
+        copy = remote(
+            ins[at].at[:, :, cols],
+            outs[at].at[depth, core, :, :, cols],
+            sends_c,
+            recvs_c,
+            u * depths,
+            sibling,
+        )
+        copy.start()
+        sent.append(copy)
+
+    def spread(u):
+        at, low, size = units[u]
+        cols = pl.ds(low, size)
+        for k in range(1, depths):
+            origin = (depth + depths - k) % depths
+            block = outs[at].at[origin, core, rep, :, cols]
+            index = u * (depths - 1) + k - 1
+            remote(block, block, sends_z, recvs_z, index, (rep, cp)).wait_recv()
+            for j in range(1, reps):
+                copy = remote(
+                    block,
+                    block,
+                    sends_r,
+                    recvs_r,
+                    index * (reps - 1) + j - 1,
+                    ((rep + j) % reps, cp),
+                )
+                copy.start()
+                sent.append(copy)
+
+    def pass_on(u):
+        at, low, size = units[u]
+        cols = pl.ds(low, size)
+        for k in range(1, depths):
+            origin = (depth + depths - k) % depths
+            index = u * (depths - 1) + k - 1
+            for j in range(1, reps):
+                block = outs[at].at[origin, core, (rep + reps - j) % reps, :, cols]
+                remote(
+                    block, block, sends_r, recvs_r, index * (reps - 1) + j - 1, (rep, cp)
+                ).wait_recv()
+            whole = outs[at].at[origin, core, :, :, cols]
+            copy = remote(whole, whole, sends_c, recvs_c, u * depths + k, sibling)
+            copy.start()
+            sent.append(copy)
+
+    for u in range(len(units)):
+        spread(u)
+        if u:
+            pass_on(u - 1)
+    pass_on(len(units) - 1)
+    for u, (at, low, size) in enumerate(units):
+        cols = pl.ds(low, size)
+        for k in range(depths):
+            origin = (depth + depths - k) % depths
+            block = outs[at].at[origin, 1 - core, :, :, cols]
+            remote(block, block, sends_c, recvs_c, u * depths + k, sibling).wait_recv()
+    for copy in sent:
+        copy.wait_send()
+    for copy in copies:
+        copy.wait()
+
+
+def cut(width, pieces):
+    size = width // pieces
+    if size % 128:
+        return [(0, width)]
+    return [(size * i, size) for i in range(pieces)]
+
+
+def gather_many(shards, pieces, identity):
+    reps = lax.axis_size("rep")
+    depths = lax.axis_size("cp") // 2
+    count = len(shards)
+    units = [
+        (at, low, size)
+        for at, shard in enumerate(shards)
+        for low, size in cut(shard.shape[2], pieces[at])
+    ]
+    hops = len(units) * (depths - 1)
+    dma = pltpu.SemaphoreType.DMA
+    return pl.pallas_call(
+        functools.partial(gather_kernel, units, count, reps, depths),
+        out_shape=[
+            jax.ShapeDtypeStruct((depths, 2) + shard.shape, shard.dtype) for shard in shards
+        ],
+        in_specs=[pl.BlockSpec(memory_space=pl.ANY)] * count,
+        out_specs=[pl.BlockSpec(memory_space=pl.ANY)] * count,
+        scratch_shapes=[
+            dma((hops,)),
+            dma((hops,)),
+            dma((hops * (reps - 1),)),
+            dma((hops * (reps - 1),)),
+            dma((len(units) * depths,)),
+            dma((len(units) * depths,)),
+            dma((count,)),
+        ],
+        compiler_params=pltpu.CompilerParams(collective_id=identity, has_side_effects=True),
+    )(*shards)
+
+
+def add_into(target, index, parts):
+    total = parts[0].astype(F32)
+    for part in parts[1:]:
+        total = total + part.astype(F32)
+    target[index] = total.astype(BF16)
+
+
+def reduce_kernel(units, count, reps, depths, *refs):
+    ins = refs[:count]
+    outs = refs[count : 2 * count]
+    at = 2 * count
+    size = len(units)
+    first = refs[at : at + size]
+    second = refs[at + size : at + 2 * size]
+    third = refs[at + 2 * size : at + 3 * size]
+    own = refs[at + 3 * size : at + 4 * size]
+    sends_c, recvs_c, sends_r, recvs_r, sends_z, recvs_z, sends_g, recvs_g = refs[at + 4 * size :]
+    rep, depth, core = places()
+    cp = 2 * depth + core
+    enter(rep, depth, core, reps, depths)
+    sibling = (rep, 2 * depth + 1 - core)
+    sent = []
+    for u, (a, low, width) in enumerate(units):
+        copy = remote(
+            ins[a].at[:, 1 - core, :, :, pl.ds(low, width)],
+            first[u],
+            sends_c,
+            recvs_c,
+            u,
+            sibling,
+        )
+        copy.start()
+        sent.append(copy)
+
+    def over_core(u):
+        a, low, width = units[u]
+        remote(first[u], first[u], sends_c, recvs_c, u, sibling).wait_recv()
+
+        def step(i, carry):
+            z = i // reps
+            q = i % reps
+            add_into(
+                first[u],
+                (z, q),
+                [first[u][z, q], ins[a][z, core, q, :, low : low + width]],
+            )
+            return carry
+
+        lax.fori_loop(0, depths * reps, step, 0)
+        for k in range(1, reps):
+            target = (rep + k) % reps
+            copy = remote(
+                first[u].at[:, target],
+                second[u].at[k - 1],
+                sends_r,
+                recvs_r,
+                u * (reps - 1) + k - 1,
+                (target, cp),
+            )
+            copy.start()
+            sent.append(copy)
+
+    def over_rep(u):
+        for k in range(1, reps):
+            block = second[u].at[k - 1]
+            remote(
+                block, block, sends_r, recvs_r, u * (reps - 1) + k - 1, (rep, cp)
+            ).wait_recv()
+
+        def step(z, carry):
+            add_into(
+                own[u],
+                z,
+                [first[u][z, rep]] + [second[u][k, z] for k in range(reps - 1)],
+            )
+            return carry
+
+        lax.fori_loop(0, depths, step, 0)
+        for k in range(1, depths):
+            target = (depth + k) % depths
+            copy = remote(
+                own[u].at[target],
+                third[u].at[k - 1],
+                sends_z,
+                recvs_z,
+                u * (depths - 1) + k - 1,
+                (rep, 2 * target + core),
+            )
+            copy.start()
+            sent.append(copy)
+
+    def over_depth(u):
+        a, low, width = units[u]
+        for k in range(1, depths):
+            block = third[u].at[k - 1]
+            remote(
+                block, block, sends_z, recvs_z, u * (depths - 1) + k - 1, (rep, cp)
+            ).wait_recv()
+        total = own[u][depth].astype(F32)
+        for k in range(depths - 1):
+            total = total + third[u][k].astype(F32)
+        outs[a][rep, :, low : low + width] = total.astype(BF16)
+        block = outs[a].at[rep, :, pl.ds(low, width)]
+        for k in range(1, reps):
+            copy = remote(
+                block,
+                block,
+                sends_g,
+                recvs_g,
+                u * (reps - 1) + k - 1,
+                ((rep + k) % reps, cp),
+            )
+            copy.start()
+            sent.append(copy)
+
+    stages = (over_core, over_rep, over_depth)
+    for step in range(size + len(stages) - 1):
+        for lag, stage in enumerate(stages):
+            if 0 <= step - lag < size:
+                stage(step - lag)
+    for u, (a, low, width) in enumerate(units):
+        for k in range(1, reps):
+            block = outs[a].at[(rep + reps - k) % reps, :, pl.ds(low, width)]
+            remote(
+                block, block, sends_g, recvs_g, u * (reps - 1) + k - 1, (rep, cp)
+            ).wait_recv()
+    for copy in sent:
+        copy.wait_send()
+
+
+def reduce_many(parts, pieces, identity):
+    reps = lax.axis_size("rep")
+    depths = lax.axis_size("cp") // 2
+    count = len(parts)
+    blocks = []
+    for part in parts:
+        rows, width = part.shape
+        blocks.append(
+            part.astype(BF16).reshape(depths, 2, reps, rows // (2 * depths * reps), width)
+        )
+    units = [
+        (at, low, size)
+        for at, block in enumerate(blocks)
+        for low, size in cut(block.shape[4], pieces[at])
+    ]
+    rows = [blocks[at].shape[3] for at, _, _ in units]
+    sizes = [size for _, _, size in units]
+    dma = pltpu.SemaphoreType.DMA
+    vmem = pl.BlockSpec(memory_space=pltpu.VMEM)
+
+    def buffers(*lead):
+        return [pltpu.VMEM(lead + (r, s), BF16) for r, s in zip(rows, sizes)]
+
+    total = len(units)
+    sums = pl.pallas_call(
+        functools.partial(reduce_kernel, units, count, reps, depths),
+        out_shape=[
+            jax.ShapeDtypeStruct((reps,) + block.shape[3:], BF16) for block in blocks
+        ],
+        in_specs=[vmem] * count,
+        out_specs=[vmem] * count,
+        scratch_shapes=buffers(depths, reps)
+        + buffers(reps - 1, depths)
+        + buffers(depths - 1)
+        + buffers(depths)
+        + [dma((total,))] * 2
+        + [dma((total * (reps - 1),))] * 2
+        + [dma((total * (depths - 1),))] * 2
+        + [dma((total * (reps - 1),))] * 2,
+        compiler_params=pltpu.CompilerParams(
+            collective_id=identity, has_side_effects=True, vmem_limit_bytes=56 * 1024 * 1024
+        ),
+    )(*blocks)
+    return [total.reshape(-1, total.shape[2]).astype(F32) for total in sums]
+
+
+def blocked(shard):
+    return shard.reshape(lax.axis_size("rep"), -1, shard.shape[1])
+
+
+def divides(rows):
+    reps = lax.axis_size("rep")
+    return lax.axis_size("cp") == 8 and reps == 4 and rows % (8 * reps) == 0
+
+
 def on_device(
     tokens,
     query_weight,
@@ -175,9 +520,9 @@
     row_count = tokens.shape[1]
     width = tokens.shape[2]
     local_tokens = tokens[0]
-    w_proj = gather_all(
-        jnp.concatenate([query_weight, mixed(key_weight, value_weight)], axis=1)
-    )
+    fast = divides(query_weight.shape[0])
+    reps = lax.axis_size("rep")
+    proj_shard = jnp.concatenate([query_weight, mixed(key_weight, value_weight)], axis=1)
     small = (
         query_bias,
         value_bias,
@@ -189,7 +534,18 @@
         second_gain,
         second_shift,
     )
-    gathered = lax.all_gather(jnp.concatenate(small)[None], "cp", axis=0, tiled=True)
+    flat_small = jnp.concatenate(small)
+    if fast:
+        unit = 8 * 128 * reps
+        padded = jnp.pad(flat_small, (0, -flat_small.shape[0] % unit))
+        w_proj, gathered = gather_many(
+            (blocked(proj_shard), padded.reshape(reps, -1, 128)), (3, 1), 1
+        )
+        w_proj = w_proj.reshape(-1, proj_shard.shape[1])
+        gathered = gathered.reshape(-1, padded.shape[0])
+    else:
+        w_proj = gather_all(proj_shard)
+        gathered = lax.all_gather(flat_small[None], "cp", axis=0, tiled=True)
     vectors = []
     at = 0
     for vector in small:
@@ -210,10 +566,20 @@
     query_rows = (matmul(local_tokens, w_proj[:, :width]) + b_query).astype(BF16)
     query_scaled = query_rows * jnp.asarray(1.0 / math.sqrt(HD), BF16)
     queries = [query_scaled[:, chunk * i : chunk * (i + 1)] for i in range(CHUNKS)]
-    w_wide = gather_all(jnp.concatenate([output_weight, up_weight], axis=1))
+    wide_shard = jnp.concatenate([output_weight, up_weight], axis=1)
+    if fast:
+        wide_shard, down_shard, _ = lax.optimization_barrier(
+            (wide_shard, down_weight, pair_rows)
+        )
+        w_wide, w_down = gather_many((blocked(wide_shard), blocked(down_shard)), (2, 2), 2)
+        w_wide = w_wide.reshape(-1, wide_shard.shape[1])
+        w_down = w_down.reshape(-1, width)
+        w_wide, queries = lax.optimization_barrier((w_wide, queries))
+    else:
+        w_wide = gather_all(wide_shard)
+        w_down = gather_all(down_weight)
     w_output = w_wide[:, :width]
     w_up = w_wide[:, width:]
-    w_down = gather_all(down_weight)
 
     context_low = jnp.concatenate(
         [attend(query, pair) for query, pair in zip(queries, pairs)], axis=1
@@ -231,31 +597,40 @@
     grad_resid2, grad_gain2, grad_shift2 = pull_second(cotangent[0])
     grad_outer = grad_resid2.astype(BF16)
     grad_down_bias = column_sum(grad_outer)
-    part_down = scatter_all(over_rows(hidden_low, grad_outer))
+    part_down = over_rows(hidden_low, grad_outer).astype(BF16)
     grad_inner = pull_gelu(against(grad_outer, w_down))[0].astype(BF16)
     grad_up_bias = column_sum(grad_inner)
-    part_up = scatter_all(over_rows(first_low, grad_inner))
+    part_up = over_rows(first_low, grad_inner).astype(BF16)
     grad_first = grad_resid2 + against(grad_inner, w_up)
     grad_resid1, grad_gain1, grad_shift1 = pull_first(grad_first)
     grad_attn = grad_resid1.astype(BF16)
     grad_output_bias = column_sum(grad_attn)
-    part_output = scatter_all(over_rows(context_low, grad_attn))
+    part_output = over_rows(context_low, grad_attn).astype(BF16)
     grad_context = against(grad_attn, w_output).astype(BF16)
 
     grad_queries = []
     grad_pairs = []
+    terms = []
     for i in range(CHUNKS):
         grad_query, grad_terms = attend_back(
             queries[i], grad_context[:, chunk * i : chunk * (i + 1)], pairs[i]
         )
         grad_queries.append(grad_query)
+        terms.append(grad_terms)
         grad_pairs.append(
             lax.psum_scatter(grad_terms, "cp", scatter_dimension=0, tiled=True)
+        )
+    if fast:
+        part_down, part_up, part_output, _ = lax.optimization_barrier(
+            (part_down, part_up, part_output, terms)
+        )
+        full_down, full_up, full_output = reduce_many(
+            (part_down, part_up, part_output), (2, 2, 1), 3
         )
     grad_query_low = jnp.concatenate(grad_queries, axis=1)
     grad_pair_low = jnp.concatenate(grad_pairs, axis=1)
     grad_proj = jnp.concatenate([grad_query_low, grad_pair_low], axis=1)
-    part_proj = scatter_all(over_rows(local_tokens, grad_proj))
+    part_proj = over_rows(local_tokens, grad_proj).astype(BF16)
     grad_tokens = grad_resid1 + against(grad_proj, w_proj)
     proj_sums = column_sum(grad_proj)
     _, grad_value_bias = unmixed(proj_sums[None, width:])
@@ -285,10 +660,13 @@
     entries = lax.axis_size("rep") * lax.axis_size("cp") * row_count * width
     rms_values = jnp.sqrt(sums[at:] / entries)
 
-    full_down, full_up, full_output, full_proj = [
-        part.astype(F32)
-        for part in lax.psum((part_down, part_up, part_output, part_proj), "rep")
-    ]
+    if fast:
+        (full_proj,) = reduce_many((part_proj,), (3,), 4)
+    else:
+        shards = [scatter_all(part) for part in (part_down, part_up, part_output, part_proj)]
+        full_down, full_up, full_output, full_proj = [
+            part.astype(F32) for part in lax.psum(tuple(shards), "rep")
+        ]
     grad_key_weight, grad_value_weight = unmixed(full_proj[:, width:])
     return (
         layer_out[None],

time: 684 us -> 436 us (0.64)
  waiting for transfers between devices: 475 us -> 29.5 us
  Pallas kernels: 52.7 us -> 273 us
  blocking collectives: 54.4 us -> 39.9 us
  local copies, waits for them, and re-layouts: 31.8 us -> 23.5 us
    pallas_call x0 -> x4, Pallas kernels: none -> 220 us  [the longest x2 127 us: reduce_many(): pl.pallas_call(functools.partial(reduce_kernel, units, count, reps, depth...]
    reduce_scatter x3 -> x0, waiting for transfers between devices: 143 us -> none  [scatter_all(): lax.psum_scatter(values.astype(BF16), 'cp', scatter_dimension=0, tiled=True)]
    all_gather x3 -> x0, waiting for transfers between devices: 128 us -> none  [gather_all(): return lax.all_gather(shard, 'cp', axis=0, tiled=True)]
    reduce_scatter x3, waiting for transfers between devices: 80.1 us -> 0.04 us  [on_device(): lax.psum_scatter(grad_terms, 'cp', scatter_dimension=0, tiled=True)]
    all_gather x3, waiting for transfers between devices: 70.5 us -> 28 us  [on_device(): lax.all_gather(pair_rows[:, 2 * chunk * i:2 * chunk * (i + 1)], 'cp', axi...]
    unnamed x15 -> x6, waiting for transfers between devices: 30.2 us -> 1.44 us
    psum x1 -> x0, waiting for transfers between devices: 22.6 us -> none  [on_device(): lax.psum((part_down, part_up, part_output, part_proj), 'rep')]
    all_gather x1 -> x0, blocking collectives: 15.8 us -> none  [on_device(): lax.all_gather(jnp.concatenate(small)[None], 'cp', axis=0, tiled=True)]
  transfers between devices with their start and end apart: 14 -> 6, of which waited for: 14 -> 2; matrix products, arithmetic and copies ran while one was open for 6% -> 5% of each run, Pallas kernels for 6% -> 44%
where the time goes in v3:
time: 436 us; the launch traced here: 432 us
  Pallas kernels  273 us (63%)
  blocking collectives  39.9 us (9%)
  matrix products  35.1 us (8%)
  waiting for transfers between devices  29.5 us (7%)
  local copies, waits for them, and re-layouts  23.5 us (5%)
  between operations  16.8 us (4%)
  other arithmetic  13.7 us (3%)
    pallas_call x2, Pallas kernels, reduce_many(): pl.pallas_call(functools.partial(reduce_kernel, units, count, reps, depth...  127 us
    pallas_call x2, Pallas kernels, gather_many(): pl.pallas_call(functools.partial(gather_kernel, units, count, reps, depth...  93.2 us
    psum x1, blocking collectives, on_device(): sums = lax.psum(flat, ('rep', 'cp'))  39.9 us
    pallas_call x3, Pallas kernels, attend_back(): pl.pallas_call(backward_kernel, grid=(width // PAIR,), in_specs=[column_b...  33.7 us
    all_gather x3, waiting for transfers between devices, on_device(): lax.all_gather(pair_rows[:, 2 * chunk * i:2 * chunk * (i + 1)], 'cp', axi...  28 us
    pallas_call x3, Pallas kernels, attend(): pl.pallas_call(forward_kernel, grid=(width // PAIR,), in_specs=[column_bl...  19.3 us
    dot_general x4, matrix products, over_rows(): lax.dot_general(left, right, (((0,), (0,)), ((), ())), preferred_element_...  12.9 us
    dot_general x5, matrix products, matmul(): return jnp.dot(left, right, preferred_element_type=F32)  11.5 us
  transfers between devices with their start and end apart: 6, of which 2 were waited for; matrix products, arithmetic and copies ran while one was open for 5% of the time, Pallas kernels for 44%

profile of v3, /device:TPU:0, one launch (start us, length us, event | category | flops | bytes accessed | tf_op | source)
XLA Modules:
  0.0 431.7 jit_solution(16787505262827640060)
XLA Ops:
  7.2 1.1 stack_reshape.8
  8.4 1.1 stack_reshape.7
  9.6 0.4 copy.46
  10.1 6.1 %concatenate.27 = bf16[1152]{0:T(1024)(128)(2,1)S(1)} concatenate(bf16[96]{0:T(256)(128)(2,1)} %param.19, bf16[96]{0:T(256)(128)(2,1)} %param.22, bf16[96]{0:T(256)(128)(2,1)} %param.24, bf16[96]{0:T(256)(128)(2,1)} %param.25, bf16[96]{0:T(256)(128)(2,1)} %param.26, bf16[384]{0:T(512)(128)(2,1)} %param.28, bf16[96]{0:T(256)(128)(2,1)} %param.30, bf16[96]{0:T(256)(128)(2,1)} %param.31, ...), dimensions={0} | concatenate | bytes 4608 | tf_op jit(solution)/shard_map/concatenate | solution.py:537
  16.2 0.6 pad_bitcast_fusion.refs_1_
  16.8 1.7 pad_maximum_fusion.1.refs_0_
  18.5 28.9 %shard_map.304 = (bf16[4,2,4,24,2304]{4,3,2,1,0:T(8,128)(2,1)}, bf16[4,2,4,8,128]{4,3,2,1,0:T(8,128)(2,1)}) custom-call(bf16[4,24,2304]{2,1,0:T(8,128)(2,1)} %pad_maximum_fusion.1.refs_0_, bf16[4,8,128]{2,1,0:T(8,128)(2,1)} %pad_bitcast_fusion.refs_1_), custom_call_target="tpu_custom_call" | custom-call | tf_op jit(solution)/shard_map/pallas_call | solution.py:296
  47.4 0.9 reshape.230
  48.5 2.5 fusion.8
  51.0 0.9 fusion.34
  52.0 0.7 all-gather.6.cloned.1.call-update
  52.8 0.7 all-gather.4.cloned.1.call-update
  53.7 0.9 pad_maximum_fusion
  54.6 64.3 %shard_map.305 = (bf16[4,2,4,24,3840]{4,3,2,1,0:T(8,128)(2,1)}, bf16[4,2,4,96,768]{4,3,2,1,0:T(8,128)(2,1)}) custom-call(bf16[4,24,3840]{2,1,0:T(8,128)(2,1)} %bitcast.80, bf16[4,96,768]{2,1,0:T(8,128)(2,1)} %bitcast.84), custom_call_target="tpu_custom_call" | custom-call | tf_op jit(solution)/shard_map/pallas_call | solution.py:296
  119.0 1.8 fusion.17
  120.8 0.8 fusion.36
  121.9 6.6 %shard_map.308 = bf16[256,256]{1,0:T(8,128)(2,1)} custom-call(bf16[256,256]{1,0:T(8,128)(2,1)} %get-tuple-element.47.query_ref, bf16[2048,512]{1,0:T(8,128)(2,1)} %all-gather.8.cloned.1.call-done.pair_ref), custom_call_target="tpu_custom_call" | custom-call | tf_op jit(solution)/shard_map/pallas_call | solution.py:108
  128.5 3.7 all-gather.6.cloned.1.call-done.pair_ref
  132.2 6.4 %shard_map.307 = bf16[256,256]{1,0:T(8,128)(2,1)} custom-call(bf16[256,256]{1,0:T(8,128)(2,1)} %get-tuple-element.46.query_ref, bf16[2048,512]{1,0:T(8,128)(2,1)} %all-gather.6.cloned.1.call-done.pair_ref), custom_call_target="tpu_custom_call" | custom-call | tf_op jit(solution)/shard_map/pallas_call | solution.py:108
  138.5 24.4 %all-gather.4.cloned.1.call-done.pair_ref = bf16[2048,512]{1,0:T(8,128)(2,1)} async-done(((bf16[256,512]{1,0:T(8,128)(2,1)}), bf16[2048,512]{1,0:T(8,128)(2,1)}) %all-gather.4.cloned.1.call-update) | async-done | bytes 2097168 | tf_op jit(solution)/shard_map/all_gather | solution.py:561
  162.9 6.4 %shard_map.306 = bf16[256,256]{1,0:T(8,128)(2,1)} custom-call(bf16[256,256]{1,0:T(8,128)(2,1)} %get-tuple-element.45.query_ref, bf16[2048,512]{1,0:T(8,128)(2,1)} %all-gather.4.cloned.1.call-done.pair_ref), custom_call_target="tpu_custom_call" | custom-call | tf_op jit(solution)/shard_map/pallas_call | solution.py:108
  169.3 2.0 fusion.38
  171.3 0.2 multiply_reduce_fusion.5
  171.5 3.7 multiply_convert_fusion
  175.3 1.5 fusion.39
  176.8 0.2 multiply_reduce_fusion.4
  177.1 0.3 fusion.21
  177.4 1.2 fusion.33
  178.7 0.7 convert_reduce_fusion.2
  179.4 3.3 convert_reduce_fusion
  182.8 2.2 multiply_reduce_fusion.1
  185.0 0.3 fusion.32
  185.4 0.8 copy-done.1
  186.2 0.7 convert_reduce_fusion.3
  186.9 0.5 convolution_convert_fusion.4
  187.5 0.8 fusion.35
  188.3 11.1 %shard_map.309 = (bf16[256,256]{1,0:T(8,128)(2,1)}, bf16[2048,512]{1,0:T(8,128)(2,1)}) custom-call(bf16[256,256]{1,0:T(8,128)(2,1)} %get-tuple-element.45.query_ref, bf16[256,256]{1,0:T(8,128)(2,1)} %get-tuple-element.85.grad_ref, bf16[2048,512]{1,0:T(8,128)(2,1)} %all-gather.4.cloned.1.call-done.pair_ref), custom_call_target="tpu_custom_call" | custom-call | tf_op jit(solution)/shard_map/pallas_call | solution.py:120
  199.4 11.1 %shard_map.310 = (bf16[256,256]{1,0:T(8,128)(2,1)}, bf16[2048,512]{1,0:T(8,128)(2,1)}) custom-call(bf16[256,256]{1,0:T(8,128)(2,1)} %get-tuple-element.46.query_ref, bf16[256,256]{1,0:T(8,128)(2,1)} %get-tuple-element.84.grad_ref, bf16[2048,512]{1,0:T(8,128)(2,1)} %all-gather.6.cloned.1.call-done.pair_ref), custom_call_target="tpu_custom_call" | custom-call | tf_op jit(solution)/shard_map/pallas_call | solution.py:120
  210.6 11.5 %shard_map.311 = (bf16[256,256]{1,0:T(8,128)(2,1)}, bf16[2048,512]{1,0:T(8,128)(2,1)}) custom-call(bf16[256,256]{1,0:T(8,128)(2,1)} %get-tuple-element.47.query_ref, bf16[256,256]{1,0:T(8,128)(2,1)} %get-tuple-element.83.grad_ref, bf16[2048,512]{1,0:T(8,128)(2,1)} %all-gather.8.cloned.1.call-done.pair_ref), custom_call_target="tpu_custom_call" | custom-call | tf_op jit(solution)/shard_map/pallas_call | solution.py:120
  222.2 0.7 reduce_sum.200
  222.8 2.7 convolution_convert_fusion.3
  225.6 3.6 convolution_convert_fusion.1
  229.1 3.7 convolution_convert_fusion
  232.9 89.0 %shard_map.313 = (bf16[4,96,768]{2,1,0:T(8,128)(2,1)}, bf16[4,24,3072]{2,1,0:T(8,128)(2,1)}, bf16[4,24,768]{2,1,0:T(8,128)(2,1)}) custom-call(bf16[4,2,4,96,768]{4,3,2,1,0:T(8,128)(2,1)} %bitcast.77, bf16[4,2,4,24,3072]{4,3,2,1,0:T(8,128)(2,1)} %bitcast.78, bf16[4,2,4,24,768]{4,3,2,1,0:T(8,128)(2,1)} %bitcast.83), custom_call_target="tpu_custom_call" | custom-call | tf_op jit(solution)/shard_map/pallas_call | solution.py:470
  322.0 1.7 bitcast_convert_fusion.3
  323.8 2.2 bitcast_convert_fusion
  325.9 1.2 bitcast_convert_fusion.1
  327.1 1.0 constant_dynamic-update-slice_fusion.2
  328.1 1.0 constant_dynamic-update-slice_fusion.1
  329.1 1.0 constant_dynamic-update-slice_fusion
  330.1 4.6 %multiply_reduce_fusion = (f32[]{:T(128)}, f32[256,768]{1,0:T(8,128)}) fusion(bf16[256,2304]{1,0:T(8,128)(2,1)S(1)} %constant_dynamic-update-slice_fusion, bf16[768,2304]{1,0:T(8,128)(2,1)} %bitcast.98, f32[256,768]{1,0:T(8,128)S(1)} %copy-done.2, f32[256]{0:T(256)S(1)} %copy-done.25), kind=kOutput, calls=%fused_computation.37 | convolution fusion | flops 906756096 | bytes 6292484 | tf_op jit(solution)/shard_map/dot_general | solution.py:39
  334.7 2.9 convolution_convert_fusion.2
  337.6 0.2 convert_reduce_fusion.1
  337.9 37.6 %shard_map.312 = bf16[4,24,2304]{2,1,0:T(8,128)(2,1)} custom-call(bf16[4,2,4,24,2304]{4,3,2,1,0:T(8,128)(2,1)} %bitcast.79), custom_call_target="tpu_custom_call" | custom-call | tf_op jit(solution)/shard_map/pallas_call | solution.py:470
  375.5 1.1 bitcast_convert_fusion.2
  376.6 0.7 slice.140
  377.6 0.6 constant_dynamic-update-slice_fusion.8
  378.3 39.9 %psum.7 = f32[9217]{0:T(1024)S(1)} all-reduce(f32[9217]{0:T(1024)S(1)} %constant_dynamic-update-slice_fusion.8), channel_id=1, replica_groups=mesh['rep'=4,'cp'=8] {'rep','cp'}, use_global_device_ids=true, to_apply=%region_20.21 | all-reduce | flops 9217 | bytes 73736 | tf_op jit(solution)/shard_map/psum | solution.py:650
  418.2 0.4 reshape.236
  418.5 1.6 slice_reduce_fusion
  420.1 0.5 slice.147
  420.6 0.7 dynamic_slice.32
  422.0 0.9 copy_bitcast_fusion
  422.9 0.6 fusion.37
  (116 shorter events, 1.7 us)
Async XLA Ops:
  7.2 41.3 %copy-start.7 = (bf16[1,256,768]{2,1,0:T(8,128)(2,1)S(1)}, bf16[1,256,768]{2,1,0:T(8,128)(2,1)}, u32[]{:S(2)}) copy-start(bf16[1,256,768]{2,1,0:T(8,128)(2,1)} %param.17) | copy-start | bytes 1179652
  7.2 114.7 %all-gather.8.cloned.1.call-start = ((), (), s32[]{:S(2)}) async-start(), calls=%async_computation.5 | async-start | bytes 2359296 | tf_op jit(solution)/shard_map/all_gather | solution.py:561
  48.5 5.1 %copy-start.6 = (bf16[96,3072]{1,0:T(8,128)(2,1)S(1)}, bf16[96,3072]{1,0:T(8,128)(2,1)}, u32[]{:S(2)}) copy-start(bf16[96,3072]{1,0:T(8,128)(2,1)} %param.27) | copy-start | bytes 1769476
  48.5 5.1 %copy-start.10 = (bf16[96,768]{1,0:T(8,128)(2,1)S(1)}, bf16[96,768]{1,0:T(8,128)(2,1)}, u32[]{:S(2)}) copy-start(bf16[96,768]{1,0:T(8,128)(2,1)} %param.23) | copy-start | bytes 442372
  52.0 80.2 %all-gather.6.cloned.1.call-start = ((), (), s32[]{:S(2)}) async-start(), calls=%async_computation.4 | async-start | bytes 2359296 | tf_op jit(solution)/shard_map/all_gather | solution.py:561
  52.7 110.2 %all-gather.4.cloned.1.call-start = ((), (), s32[]{:S(2)}) async-start(), calls=%async_computation.3 | async-start | bytes 2359296 | tf_op jit(solution)/shard_map/all_gather | solution.py:561
  53.4 273.6 %reduce-scatter.4.cloned.1.call-start = ((), (), s32[]{:S(2)}) async-start(), calls=%async_computation.6 | async-start | bytes 2359296 | tf_op jit(solution)/shard_map/reduce_scatter | solution.py:621
  128.5 40.8 %copy-start.11 = (bf16[256,256]{1,0:T(8,128)(2,1)S(1)}, bf16[256,256]{1,0:T(8,128)(2,1)}, u32[]{:S(2)}) copy-start(bf16[256,256]{1,0:T(8,128)(2,1)} %shard_map.308) | copy-start | bytes 393220
  171.3 4.0 slice-start.2
  171.5 13.5 %copy-start.19 = (f32[256]{0:T(256)}, f32[256]{0:T(256)S(1)}, u32[]{:S(2)}) copy-start(f32[256]{0:T(256)S(1)} %fusion.26) | copy-start | bytes 3076
  171.5 3.8 slice-start.3
  175.3 1.8 copy-start
  178.7 4.1 slice-start
  179.4 3.4 slice-start.1
  182.8 2.2 copy-start.3
  185.3 0.9 copy-start.1
  185.4 1.6 copy-start.24
  186.9 1.3 copy-start.9
  199.4 128.7 %reduce-scatter.6.cloned.1.call-start = ((), (), s32[]{:S(2)}) async-start(), calls=%async_computation.7 | async-start | bytes 2359296 | tf_op jit(solution)/shard_map/reduce_scatter | solution.py:621
  210.6 118.5 %reduce-scatter.8.cloned.1.call-start = ((), (), s32[]{:S(2)}) async-start(), calls=%async_computation.8 | async-start | bytes 2359296 | tf_op jit(solution)/shard_map/reduce_scatter | solution.py:621
  225.5 3.6 copy-start.4
  225.6 3.6 copy-start.20
  232.9 89.1 %copy-start.12 = (bf16[256,256]{1,0:T(8,128)(2,1)S(1)}, bf16[256,256]{1,0:T(8,128)(2,1)}, u32[]{:S(2)}) copy-start(bf16[256,256]{1,0:T(8,128)(2,1)} %get-tuple-element.50) | copy-start | bytes 393220
  232.9 89.1 %copy-start.13 = (bf16[256,256]{1,0:T(8,128)(2,1)S(1)}, bf16[256,256]{1,0:T(8,128)(2,1)}, u32[]{:S(2)}) copy-start(bf16[256,256]{1,0:T(8,128)(2,1)} %get-tuple-element.51) | copy-start | bytes 393220
  232.9 89.1 %copy-start.14 = (bf16[256,256]{1,0:T(8,128)(2,1)S(1)}, bf16[256,256]{1,0:T(8,128)(2,1)}, u32[]{:S(2)}) copy-start(bf16[256,256]{1,0:T(8,128)(2,1)} %get-tuple-element.52) | copy-start | bytes 393220
  321.9 4.0 copy-start.5
  321.9 8.1 %copy-start.2 = (f32[256,768]{1,0:T(8,128)S(1)}, f32[256,768]{1,0:T(8,128)}, u32[]{:S(2)}) copy-start(f32[256,768]{1,0:T(8,128)} %copy-done.1) | copy-start | bytes 2359300
  321.9 8.1 %copy-start.25 = (f32[256]{0:T(256)S(1)}, f32[256]{0:T(256)}, u32[]{:S(2)}) copy-start(f32[256]{0:T(256)} %copy-done.24) | copy-start | bytes 3076
  330.1 4.7 %copy-start.8 = (bf16[1,256,768]{2,1,0:T(8,128)(2,1)S(1)}, bf16[1,256,768]{2,1,0:T(8,128)(2,1)}, u32[]{:S(2)}) copy-start(bf16[1,256,768]{2,1,0:T(8,128)(2,1)} %param.17) | copy-start | bytes 1179652
  337.8 39.6 %copy-start.15 = (f32[9217]{0:T(1024)S(1)}, f32[9217]{0:T(1024)}, u32[]{:S(2)}) copy-start(f32[9217]{0:T(1024)} %custom-call) | copy-start | bytes 110608
  337.8 39.7 %copy-start.17 = (f32[768]{0:T(1024)S(1)}, f32[768]{0:T(1024)}, u32[]{:S(2)}) copy-start(f32[768]{0:T(1024)} %get-tuple-element.73) | copy-start | bytes 9220
  337.8 39.7 %copy-start.23 = (f32[768]{0:T(1024)S(1)}, f32[768]{0:T(1024)}, u32[]{:S(2)}) copy-start(f32[768]{0:T(1024)} %get-tuple-element.64) | copy-start | bytes 9220
  337.8 39.7 %copy-start.22 = (f32[768]{0:T(1024)S(1)}, f32[768]{0:T(1024)}, u32[]{:S(2)}) copy-start(f32[768]{0:T(1024)} %get-tuple-element.66) | copy-start | bytes 9220
  337.8 39.7 %copy-start.21 = (f32[3072]{0:T(1024)S(1)}, f32[3072]{0:T(1024)}, u32[]{:S(2)}) copy-start(f32[3072]{0:T(1024)} %get-tuple-element.71) | copy-start | bytes 36868
  337.8 39.7 %copy-start.16 = (f32[768]{0:T(1024)S(1)}, f32[768]{0:T(1024)}, u32[]{:S(2)}) copy-start(f32[768]{0:T(1024)} %get-tuple-element.69) | copy-start | bytes 9220
  337.9 39.7 %copy-start.18 = (f32[768]{0:T(1024)S(1)}, f32[768]{0:T(1024)}, u32[]{:S(2)}) copy-start(f32[768]{0:T(1024)} %reduce_sum.200) | copy-start | bytes 9220
Sparse Core Ops, SparseCore 0:
  52.1 48.7 all-gather.7
  103.0 29.0 all-gather.5
  134.3 28.5 all-gather.3
  199.5 35.2 reduce-scatter.3
  236.9 37.4 reduce-scatter.5
  276.6 43.5 reduce-scatter.7
